TPU v7x, 32 devices: a whole 2x2x4 slice. The times are simulated.
32 devices in a mesh: af: 4 (over y, x), sa: 8 (over z, core).
Axes of the slice: x: 2, y: 2, z: 4, core: 2. Of those that a mesh axis runs over, the one named last changes fastest.
Arguments:
- data_real: bfloat16 [64, 512, 512], P('af', 'sa'), may hold values from -0.5 to 0.5
- data_imaginary: bfloat16 [64, 512, 512], P('af', 'sa'), may hold values from -0.5 to 0.5
- wavelet_real: float32 [64], P('af'), may hold values from -2.5 to 2.5
- wavelet_imaginary: float32 [64], P('af'), may hold values from -2.5 to 2.5
- primaries_real: float32 [64, 512, 512], P('af', 'sa'), may hold values from -3 to 3
- primaries_imaginary: float32 [64, 512, 512], P('af', 'sa'), may hold values from -3 to 3
Outputs:
- updated_real: float32 [64, 512, 512], P('af', 'sa')
- updated_imaginary: float32 [64, 512, 512], P('af', 'sa')
- misfit: float32 [2], replicated
All inputs are finite; a program needn't handle non-finite values.
Results may differ from a plain program's by a relative error of at most 0.0018.
Values may be sent and summed in bfloat16 or wider, within the bound.
No kernel may reach another device: no remote copies, remote signals or barrier semaphores. Data moves between devices by JAX's collectives and lax.ppermute only.
A program may use at most 128 MiB of HBM per device.

v0:
```python
import math

import jax
import jax.numpy as jnp
from jax import lax
from jax.sharding import PartitionSpec as P

N = 512
F = 64
ITERS = 2


STEP_LENGTH = 0.02
THRESHOLD = 0.25


def fourier_tables(row_index, col_index):
    phase = row_index[:, None] * col_index[None, :] % F
    angle = phase.astype(jnp.float32) * (2.0 * math.pi / F)
    factor = 1.0 / math.sqrt(F)
    return (jnp.cos(angle) * factor, jnp.sin(angle) * factor)


def highest(left, right):
    return jnp.dot(left, right, precision=lax.Precision.HIGHEST, preferred_element_type=jnp.float32)


def stacked(part_real, part_imaginary):
    return jnp.concatenate(
        [part_real.astype(jnp.bfloat16), part_imaginary.astype(jnp.bfloat16)], axis=1
    )


def shrink(values):
    return values - jnp.clip(values, -THRESHOLD, THRESHOLD)


def on_device(
    data_real, data_imaginary, wavelet_real, wavelet_imaginary, primaries_real, primaries_imaginary
):
    row_count = data_real.shape[1]
    wave_real = wavelet_real[:, None, None]
    wave_imaginary = wavelet_imaginary[:, None, None]
    current_real = primaries_real
    current_imaginary = primaries_imaginary
    own_real = data_real.astype(jnp.float32)
    own_imaginary = data_imaginary.astype(jnp.float32)
    whole_real, whole_imaginary = (
        lax.all_gather(data_real, "sa", axis=1, tiled=True),
        lax.all_gather(data_imaginary, "sa", axis=1, tiled=True),
    )
    local_sums = []
    for iteration in range(ITERS):
        left_rows = stacked(current_real, current_imaginary)
        product_real = jnp.einsum(
            "frk,fkc->frc", left_rows, whole_real, preferred_element_type=jnp.float32
        )
        product_imaginary = jnp.einsum(
            "frk,fkc->frc", left_rows, whole_imaginary, preferred_element_type=jnp.float32
        )
        forward_real = product_real[:, :row_count] - product_imaginary[:, row_count:]
        forward_imaginary = product_imaginary[:, :row_count] + product_real[:, row_count:]
        error_real = (
            own_real
            + forward_real
            - (wave_real * current_real - wave_imaginary * current_imaginary)
        )
        error_imaginary = (
            own_imaginary
            + forward_imaginary
            - (wave_real * current_imaginary + wave_imaginary * current_real)
        )
        local_sum = jnp.sum(error_real * error_real) + jnp.sum(error_imaginary * error_imaginary)
        local_sums.append(local_sum)
        error_rows = stacked(error_real, error_imaginary)
        with_real = jnp.einsum(
            "frk,fjk->frj", error_rows, whole_real, preferred_element_type=jnp.float32
        )
        with_imaginary = jnp.einsum(
            "frk,fjk->frj", error_rows, whole_imaginary, preferred_element_type=jnp.float32
        )
        back_real = with_real[:, :row_count] + with_imaginary[:, row_count:]
        back_imaginary = with_real[:, row_count:] - with_imaginary[:, :row_count]
        gradient_real = wave_real * error_real + wave_imaginary * error_imaginary - back_real
        gradient_imaginary = (
            wave_real * error_imaginary - wave_imaginary * error_real - back_imaginary
        )
        stepped_real = current_real + STEP_LENGTH * gradient_real
        stepped_imaginary = current_imaginary + STEP_LENGTH * gradient_imaginary
        trace_real, trace_imaginary = (
            lax.all_to_all(stepped_real, "af", split_axis=2, concat_axis=0, tiled=True),
            lax.all_to_all(stepped_imaginary, "af", split_axis=2, concat_axis=0, tiled=True),
        )
        block_shape = trace_real.shape
        flat_real = trace_real.reshape(F, -1)
        flat_imaginary = trace_imaginary.reshape(F, -1)
        every_index = jnp.arange(F, dtype=jnp.int32)
        cosine, sine = fourier_tables(every_index, every_index)
        time_real = highest(cosine, flat_real) - highest(sine, flat_imaginary)
        time_imaginary = highest(sine, flat_real) + highest(cosine, flat_imaginary)
        shrunk_real = shrink(time_real)
        shrunk_imaginary = shrink(time_imaginary)
        freq_real = (highest(cosine, shrunk_real) + highest(sine, shrunk_imaginary)).reshape(
            block_shape
        )
        freq_imaginary = (highest(cosine, shrunk_imaginary) - highest(sine, shrunk_real)).reshape(
            block_shape
        )
        current_real, current_imaginary = (
            lax.all_to_all(freq_real, "af", split_axis=0, concat_axis=2, tiled=True),
            lax.all_to_all(freq_imaginary, "af", split_axis=0, concat_axis=2, tiled=True),
        )
    totals = lax.psum(jnp.stack(local_sums), ("af", "sa"))
    misfit = totals / (F * N * N)
    return (current_real, current_imaginary, misfit)


def solution(mesh):
    in_specs = (
        P("af", "sa", None),
        P("af", "sa", None),
        P("af"),
        P("af"),
        P("af", "sa", None),
        P("af", "sa", None),
    )
    out_specs = (P("af", "sa", None), P("af", "sa", None), P())
    return jax.shard_map(
        on_device, mesh=mesh, in_specs=in_specs, out_specs=out_specs, check_vma=False
    )
```

profile of v0, /device:TPU:0, one launch (start us, length us, event | category | flops | bytes accessed | tf_op | source)
XLA Modules:
  0.0 607.0 jit_solution(6934212573473681621)
XLA Ops:
  12.5 81.9 %all-gather.5.cloned.1.call-done = bf16[16,512,512]{2,1,0:T(8,128)(2,1)} async-done(((bf16[16,64,512]{2,1,0:T(8,128)(2,1)}), bf16[16,512,512]{2,1,0:T(8,128)(2,1)}) %all-gather.5.cloned.1.call-update) | async-done | bytes 8388624 | tf_op jit(solution)/shard_map/all_gather | solution.py:50
  94.4 7.3 %fusion.46 = f32[16,128,512]{2,1,0:T(8,128)} fusion(bf16[16,512,512]{2,1,0:T(8,128)(2,1)} %all-gather.5.cloned.1.call-done, bf16[16,64,512]{2,1,0:T(8,128)(2,1)} %convert_element_type.67, bf16[16,64,512]{2,1,0:T(8,128)(2,1)} %convert_element_type.66), kind=kOutput, calls=%fused_computation.88 | convolution fusion | flops 1077936128 | bytes 14680064 | tf_op jit(solution)/shard_map/frk,fkc->frc/dot_general | solution.py:58
  101.6 74.9 %all-gather.3.cloned.1.call-done = bf16[16,512,512]{2,1,0:T(8,128)(2,1)} async-done(((bf16[16,64,512]{2,1,0:T(8,128)(2,1)}), bf16[16,512,512]{2,1,0:T(8,128)(2,1)}) %all-gather.3.cloned.1.call-update) | async-done | bytes 8388624 | tf_op jit(solution)/shard_map/all_gather | solution.py:49
  176.5 5.4 fusion.47
  189.1 6.8 %fusion.44 = f32[16,128,512]{2,1,0:T(8,128)} fusion(bf16[16,512,512]{2,1,0:T(8,128)(2,1)S(1)} %bitcast.119, bf16[16,64,512]{2,1,0:T(8,128)(2,1)} %convert_element_type.70, bf16[16,64,512]{2,1,0:T(8,128)(2,1)} %convert_element_type.69), kind=kOutput, calls=%fused_computation.86 | convolution fusion | flops 1077936128 | bytes 14680064 | tf_op jit(solution)/shard_map/frk,fjk->frj/dot_general | solution.py:79
  195.9 6.5 %fusion.45 = f32[16,128,512]{2,1,0:T(8,128)} fusion(bf16[16,512,512]{2,1,0:T(8,128)(2,1)S(1)} %bitcast.123, bf16[16,64,512]{2,1,0:T(8,128)(2,1)} %convert_element_type.70, bf16[16,64,512]{2,1,0:T(8,128)(2,1)} %convert_element_type.69), kind=kOutput, calls=%fused_computation.87 | convolution fusion | flops 1077936128 | bytes 14680064 | tf_op jit(solution)/shard_map/frk,fjk->frj/dot_general | solution.py:76
  202.5 5.8 fusion.24
  208.3 4.9 copy.19
  213.2 5.5 reshape.44
  218.6 3.6 all-to-all-start
  222.3 4.9 copy.21
  227.2 5.5 reshape.46
  232.7 15.1 %all-to-all-done = f32[4,1,131072]{2,1,0:T(1,128)S(1)} async-done(((f32[4,1,131072]{2,1,0:T(1,128)}), f32[4,1,131072]{2,1,0:T(1,128)S(1)}, u32[]{:S(2)}, u32[]{:S(2)}) %all-to-all-start) | async-done | bytes 2097184 | tf_op jit(solution)/shard_map/all_to_all | solution.py:91
  249.1 4.6 all-to-all-start.1
  254.2 7.6 %reduce = f32[4,131072]{1,0:T(4,128)S(1)} reduce(f32[4,1,131072]{2,1,0:T(1,128)} %copy-done.27, f32[]{:T(128)} %broadcast.92), dimensions={1}, to_apply=%all_to_all.96.reduce_sub_computation | reduce | bytes 4194308 | tf_op jit(solution)/shard_map/all_to_all | solution.py:91
  261.8 3.9 reshape.45
  269.1 4.4 fusion.12
  273.5 4.4 fusion.14
  278.4 7.6 %reduce.1 = f32[4,131072]{1,0:T(4,128)S(1)} reduce(f32[4,1,131072]{2,1,0:T(1,128)} %all-to-all-done.1, f32[]{:T(128)} %broadcast.92), dimensions={1}, to_apply=%all_to_all.99.reduce_sub_computation | reduce | bytes 4194308 | tf_op jit(solution)/shard_map/all_to_all | solution.py:92
  286.0 4.4 reshape.47
  293.5 4.9 clamp_subtract_fusion.2
  307.8 3.8 all-to-all-start.3
  311.6 3.7 fusion.57
  319.2 16.7 %all-to-all-done.3 = f32[64,64,128]{2,1,0:T(8,128)S(1)} async-done(((f32[64,64,128]{2,1,0:T(8,128)}), f32[64,64,128]{2,1,0:T(8,128)S(1)}, u32[]{:S(2)}, u32[]{:S(2)}) %all-to-all-start.3) | async-done | bytes 2097184 | tf_op jit(solution)/shard_map/all_to_all | solution.py:111
  335.9 4.5 all-to-all-start.2
  341.6 23.3 %all-to-all-done.2 = f32[64,64,128]{2,1,0:T(8,128)} async-done(((f32[64,64,128]{2,1,0:T(8,128)}), f32[64,64,128]{2,1,0:T(8,128)}, u32[]{:S(2)}, u32[]{:S(2)}) %all-to-all-start.2) | async-done | bytes 2097184 | tf_op jit(solution)/shard_map/all_to_all | solution.py:110
  366.8 4.9 fusion.42
  373.4 3.8 multiply_reduce_fusion.1
  380.8 6.4 %fusion.40 = f32[16,128,512]{2,1,0:T(8,128)} fusion(bf16[16,512,512]{2,1,0:T(8,128)(2,1)S(1)} %bitcast.121, bf16[16,64,512]{2,1,0:T(8,128)(2,1)} %convert_element_type.74, bf16[16,64,512]{2,1,0:T(8,128)(2,1)} %convert_element_type.73), kind=kOutput, calls=%fused_computation.82 | convolution fusion | flops 1077936128 | bytes 14680064 | tf_op jit(solution)/shard_map/frk,fjk->frj/dot_general | solution.py:79
  387.2 6.5 %fusion.41 = f32[16,128,512]{2,1,0:T(8,128)} fusion(bf16[16,512,512]{2,1,0:T(8,128)(2,1)S(1)} %bitcast.125, bf16[16,64,512]{2,1,0:T(8,128)(2,1)} %convert_element_type.74, bf16[16,64,512]{2,1,0:T(8,128)(2,1)} %convert_element_type.73), kind=kOutput, calls=%fused_computation.83 | convolution fusion | flops 1077936128 | bytes 14680064 | tf_op jit(solution)/shard_map/frk,fjk->frj/dot_general | solution.py:76
  393.7 5.1 bitcast_add_fusion
  398.7 4.9 copy.25
  403.6 5.5 reshape.48
  412.7 4.9 copy.27
  417.6 5.5 reshape.50
  423.1 13.9 %all-to-all-done.4 = f32[4,1,131072]{2,1,0:T(1,128)S(1)} async-done(((f32[4,1,131072]{2,1,0:T(1,128)}), f32[4,1,131072]{2,1,0:T(1,128)S(1)}, u32[]{:S(2)}, u32[]{:S(2)}) %all-to-all-start.4) | async-done | bytes 2097184 | tf_op jit(solution)/shard_map/all_to_all | solution.py:91
  438.4 4.7 all-to-all-start.5
  443.0 7.6 %reduce.2 = f32[4,131072]{1,0:T(4,128)S(1)} reduce(f32[4,1,131072]{2,1,0:T(1,128)} %copy-done.28, f32[]{:T(128)} %broadcast.92), dimensions={1}, to_apply=%all_to_all.110.reduce_sub_computation | reduce | bytes 4194308 | tf_op jit(solution)/shard_map/all_to_all | solution.py:91
  450.7 3.9 reshape.49
  458.1 4.4 fusion.6
  462.5 4.4 fusion.8
  467.5 7.6 %reduce.3 = f32[4,131072]{1,0:T(4,128)S(1)} reduce(f32[4,1,131072]{2,1,0:T(1,128)} %all-to-all-done.5, f32[]{:T(128)} %broadcast.92), dimensions={1}, to_apply=%all_to_all.113.reduce_sub_computation | reduce | bytes 4194308 | tf_op jit(solution)/shard_map/all_to_all | solution.py:92
  475.1 4.1 reshape.51
  482.3 4.9 clamp_subtract_fusion
  496.5 4.8 all-to-all-start.6
  507.3 18.5 %all-to-all-done.6 = f32[64,64,128]{2,1,0:T(8,128)} async-done(((f32[64,64,128]{2,1,0:T(8,128)}), f32[64,64,128]{2,1,0:T(8,128)}, u32[]{:S(2)}, u32[]{:S(2)}) %all-to-all-start.6) | async-done | bytes 2097184 | tf_op jit(solution)/shard_map/all_to_all | solution.py:110
  531.9 54.3 %psum.7 = f32[2]{0:T(128)S(1)} all-reduce(f32[2]{0:T(128)S(1)} %pad_maximum_fusion.12), channel_id=1, replica_groups=mesh['af'=4,'sa'=8] {'af','sa'}, use_global_device_ids=true, to_apply=%region_4.5 | all-reduce | flops 2 | bytes 16 | tf_op jit(solution)/shard_map/psum | solution.py:113
  586.7 4.3 copy.90
  (124 shorter events, 82.6 us)
Async XLA Ops:
  7.2 87.2 %all-gather.5.cloned.1.call-start = ((), (), s32[]{:S(2)}) async-start(), calls=%async_computation.9 | async-start | bytes 9437184 | tf_op jit(solution)/shard_map/all_gather | solution.py:50
  7.9 3.5 copy-start.8
  7.9 168.6 %all-gather.3.cloned.1.call-start = ((), (), s32[]{:S(2)}) async-start(), calls=%async_computation.8 | async-start | bytes 9437184 | tf_op jit(solution)/shard_map/all_gather | solution.py:49
  101.6 80.3 %copy-start.29 = (f32[16]{0:T(128)S(1)}, f32[16]{0:T(128)}, u32[]{:S(2)}) copy-start(f32[16]{0:T(128)} %param.9) | copy-start | bytes 196
  101.6 80.3 %copy-start.30 = (f32[16]{0:T(128)S(1)}, f32[16]{0:T(128)}, u32[]{:S(2)}) copy-start(f32[16]{0:T(128)} %param.8) | copy-start | bytes 196
  176.5 5.5 copy-start
  176.5 5.9 copy-start.9
  176.5 6.1 %copy-start.21 = (bf16[16,64,512]{2,1,0:T(8,128)(2,1)S(1)}, bf16[16,64,512]{2,1,0:T(8,128)(2,1)}, u32[]{:S(2)}) copy-start(bf16[16,64,512]{2,1,0:T(8,128)(2,1)} %param.7) | copy-start | bytes 3145732
  176.5 6.4 %copy-start.23 = (bf16[16,64,512]{2,1,0:T(8,128)(2,1)S(1)}, bf16[16,64,512]{2,1,0:T(8,128)(2,1)}, u32[]{:S(2)}) copy-start(bf16[16,64,512]{2,1,0:T(8,128)(2,1)} %param.6) | copy-start | bytes 3145732
  176.5 12.5 %slice-start = ((s8[8388608]{0:T(1024)(128)(4,1)}), s8[4194304]{0:T(1024)(128)(4,1)S(1)}, s32[]{:S(2)}) async-start(s8[8388608]{0:T(1024)(128)(4,1)} %bitcast.118), calls=%async_computation.10 | async-start | bytes 8388608
  182.9 6.1 %slice-start.1 = ((s8[8388608]{0:T(1024)(128)(4,1)}), s8[4194304]{0:T(1024)(128)(4,1)S(1)}, s32[]{:S(2)}) async-start(s8[8388608]{0:T(1024)(128)(4,1)} %bitcast.118), calls=%async_computation.11 | async-start | bytes 8388608
  185.6 1.6 copy-start.15
  185.6 2.3 copy-start.17
  187.9 8.0 %slice-start.4 = ((s8[8388608]{0:T(1024)(128)(4,1)}), s8[4194304]{0:T(1024)(128)(4,1)S(1)}, s32[]{:S(2)}) async-start(s8[8388608]{0:T(1024)(128)(4,1)} %bitcast.122), calls=%async_computation.14 | async-start | bytes 8388608
  189.0 6.8 %slice-start.5 = ((s8[8388608]{0:T(1024)(128)(4,1)}), s8[4194304]{0:T(1024)(128)(4,1)S(1)}, s32[]{:S(2)}) async-start(s8[8388608]{0:T(1024)(128)(4,1)} %bitcast.122), calls=%async_computation.15 | async-start | bytes 8388608
  195.9 6.6 %copy-start.10 = (f32[16,64,512]{2,1,0:T(8,128)S(1)}, f32[16,64,512]{2,1,0:T(8,128)}, u32[]{:S(2)}) copy-start(f32[16,64,512]{2,1,0:T(8,128)} %param.10) | copy-start | bytes 6291460
  195.9 6.6 %copy-start.16 = (f32[16,64,512]{2,1,0:T(8,128)S(1)}, f32[16,64,512]{2,1,0:T(8,128)}, u32[]{:S(2)}) copy-start(f32[16,64,512]{2,1,0:T(8,128)} %copy-done.15) | copy-start | bytes 6291460
  195.9 6.5 %copy-start.18 = (f32[16,64,512]{2,1,0:T(8,128)S(1)}, f32[16,64,512]{2,1,0:T(8,128)}, u32[]{:S(2)}) copy-start(f32[16,64,512]{2,1,0:T(8,128)} %copy-done.17) | copy-start | bytes 6291460
  218.6 29.1 %all-to-all-start = ((f32[4,1,131072]{2,1,0:T(1,128)}), f32[4,1,131072]{2,1,0:T(1,128)S(1)}, u32[]{:S(2)}, u32[]{:S(2)}) async-start(f32[4,1,131072]{2,1,0:T(1,128)} %reshape.44), calls=%async_computation | async-start | bytes 4194304 | tf_op jit(solution)/shard_map/all_to_all | solution.py:91
  247.8 1.3 copy-start.27
  249.1 29.3 %all-to-all-start.1 = ((f32[4,1,131072]{2,1,0:T(1,128)}), f32[4,1,131072]{2,1,0:T(1,128)}, u32[]{:S(2)}, u32[]{:S(2)}) async-start(f32[4,1,131072]{2,1,0:T(1,128)} %reshape.46), calls=%async_computation.1 | async-start | bytes 4194304 | tf_op jit(solution)/shard_map/all_to_all | solution.py:92
  293.5 5.0 copy-start.26
  298.5 3.3 copy-start.1
  301.8 6.0 copy-start.7
  307.8 28.2 %all-to-all-start.3 = ((f32[64,64,128]{2,1,0:T(8,128)}), f32[64,64,128]{2,1,0:T(8,128)S(1)}, u32[]{:S(2)}, u32[]{:S(2)}) async-start(f32[64,64,128]{2,1,0:T(8,128)} %bitcast.150), calls=%async_computation.3 | async-start | bytes 4194304 | tf_op jit(solution)/shard_map/all_to_all | solution.py:111
  311.6 3.8 copy-start.2
  335.9 28.9 %all-to-all-start.2 = ((f32[64,64,128]{2,1,0:T(8,128)}), f32[64,64,128]{2,1,0:T(8,128)}, u32[]{:S(2)}, u32[]{:S(2)}) async-start(f32[64,64,128]{2,1,0:T(8,128)} %bitcast.152), calls=%async_computation.2 | async-start | bytes 4194304 | tf_op jit(solution)/shard_map/all_to_all | solution.py:110
  364.9 1.9 copy-start.20
  364.9 6.9 %slice-start.6 = ((s8[8388608]{0:T(1024)(128)(4,1)}), s8[4194304]{0:T(1024)(128)(4,1)S(1)}, s32[]{:S(2)}) async-start(s8[8388608]{0:T(1024)(128)(4,1)} %bitcast.124), calls=%async_computation.16 | async-start | bytes 8388608
  366.8 5.1 slice-start.7
  371.9 1.5 copy-start.24
  371.9 8.9 %slice-start.2 = ((s8[8388608]{0:T(1024)(128)(4,1)}), s8[4194304]{0:T(1024)(128)(4,1)S(1)}, s32[]{:S(2)}) async-start(s8[8388608]{0:T(1024)(128)(4,1)} %bitcast.120), calls=%async_computation.12 | async-start | bytes 8388608
  373.4 7.4 %slice-start.3 = ((s8[8388608]{0:T(1024)(128)(4,1)}), s8[4194304]{0:T(1024)(128)(4,1)S(1)}, s32[]{:S(2)}) async-start(s8[8388608]{0:T(1024)(128)(4,1)} %bitcast.120), calls=%async_computation.13 | async-start | bytes 8388608
  377.2 1.3 copy-start.11
  377.2 2.4 copy-start.13
  387.2 6.5 %copy-start.12 = (f32[16,64,512]{2,1,0:T(8,128)S(1)}, f32[16,64,512]{2,1,0:T(8,128)}, u32[]{:S(2)}) copy-start(f32[16,64,512]{2,1,0:T(8,128)} %copy-done.11) | copy-start | bytes 6291460
  387.2 6.5 %copy-start.14 = (f32[16,64,512]{2,1,0:T(8,128)S(1)}, f32[16,64,512]{2,1,0:T(8,128)}, u32[]{:S(2)}) copy-start(f32[16,64,512]{2,1,0:T(8,128)} %copy-done.13) | copy-start | bytes 6291460
  387.2 6.5 %copy-start.19 = (f32[16,128,512]{2,1,0:T(8,128)S(1)}, f32[16,128,512]{2,1,0:T(8,128)}, u32[]{:S(2)}) copy-start(f32[16,128,512]{2,1,0:T(8,128)} %fusion.40) | copy-start | bytes 12582916
  409.1 28.0 %all-to-all-start.4 = ((f32[4,1,131072]{2,1,0:T(1,128)}), f32[4,1,131072]{2,1,0:T(1,128)S(1)}, u32[]{:S(2)}, u32[]{:S(2)}) async-start(f32[4,1,131072]{2,1,0:T(1,128)} %reshape.48), calls=%async_computation.4 | async-start | bytes 4194304 | tf_op jit(solution)/shard_map/all_to_all | solution.py:91
  437.0 1.3 copy-start.28
  438.4 29.1 %all-to-all-start.5 = ((f32[4,1,131072]{2,1,0:T(1,128)}), f32[4,1,131072]{2,1,0:T(1,128)}, u32[]{:S(2)}, u32[]{:S(2)}) async-start(f32[4,1,131072]{2,1,0:T(1,128)} %reshape.50), calls=%async_computation.5 | async-start | bytes 4194304 | tf_op jit(solution)/shard_map/all_to_all | solution.py:92
  482.3 5.0 copy-start.25
  487.2 5.4 copy-start.3
  490.5 2.1 copy-start.5
  496.5 4.8 copy-start.4
  496.5 29.3 %all-to-all-start.6 = ((f32[64,64,128]{2,1,0:T(8,128)}), f32[64,64,128]{2,1,0:T(8,128)}, u32[]{:S(2)}, u32[]{:S(2)}) async-start(f32[64,64,128]{2,1,0:T(8,128)} %bitcast.151), calls=%async_computation.6 | async-start | bytes 4194304 | tf_op jit(solution)/shard_map/all_to_all | solution.py:110
  501.3 2.1 copy-start.6
  525.8 68.3 %all-to-all-start.7 = ((f32[64,64,128]{2,1,0:T(8,128)}), f32[64,64,128]{2,1,0:T(8,128)S(1)}, u32[]{:S(2)}, u32[]{:S(2)}) async-start(f32[64,64,128]{2,1,0:T(8,128)} %bitcast.43), calls=%async_computation.7 | async-start | bytes 4194304 | tf_op jit(solution)/shard_map/all_to_all | solution.py:111
  (1 other events, 1.3 us)
Sparse Core Ops, SparseCore 0:
  9.6 84.7 all-gather.4
  96.0 80.5 all-gather.2
where the time goes:
time: 616 us; the launch traced here: 607 us
  waiting for transfers between devices  247 us (40%)
  local copies, waits for them, and re-layouts  101 us (16%)
  matrix products  97.7 us (16%)
  other arithmetic  56.9 us (9%)
  blocking collectives  54.3 us (9%)
  starting transfers between devices  33.3 us (5%)
  between operations  17.2 us (3%)
    all_gather x1, waiting for transfers between devices, on_device(): lax.all_gather(data_imaginary, 'sa', axis=1, tiled=True)  81.9 us
    all_gather x1, waiting for transfers between devices, on_device(): lax.all_gather(data_real, 'sa', axis=1, tiled=True)  74.9 us
    psum x1, blocking collectives, on_device(): totals = lax.psum(jnp.stack(local_sums), ('af', 'sa'))  54.3 us
    dot_general x16, matrix products, highest(): jnp.dot(left, right, precision=lax.Precision.HIGHEST, preferred_element_t...  52.7 us
    unnamed x90, local copies, waits for them, and re-layouts  51.7 us
    all_to_all x2, waiting for transfers between devices, on_device(): lax.all_to_all(freq_real, 'af', split_axis=0, concat_axis=2, tiled=True)  41.8 us
    all_to_all x2, waiting for transfers between devices, on_device(): lax.all_to_all(stepped_real, 'af', split_axis=2, concat_axis=0, tiled=True)  29.1 us
    all_to_all x2, waiting for transfers between devices, on_device(): lax.all_to_all(freq_imaginary, 'af', split_axis=0, concat_axis=2, tiled=T...  16.7 us
  transfers between devices with their start and end apart: 10, of which 9 were waited for; matrix products, arithmetic and copies ran while one was open for 16% of the time, Pallas kernels for 0%

commit v1 on v0

v1 whole, which is shorter than its diff:
```python
import math
from functools import partial

import jax
import jax.numpy as jnp
from jax import lax
from jax.experimental import pallas as pl
from jax.experimental.pallas import tpu as pltpu
from jax.sharding import PartitionSpec as P

ITERS = 2
STEP_LENGTH = 0.02
THRESHOLD = 0.25
CHUNKS = 4
TOP = 15.0
TINY = 1e-30
RADIX = 8
HALF = math.sqrt(0.5)


def add(a, b):
    return (a[0] + b[0], a[1] + b[1])


def sub(a, b):
    return (a[0] - b[0], a[1] - b[1])


def turn(a, sign):
    return (-a[1], a[0]) if sign > 0 else (a[1], -a[0])


def dft4(x, sign):
    a, b = add(x[0], x[2]), sub(x[0], x[2])
    c, d = add(x[1], x[3]), turn(sub(x[1], x[3]), sign)
    return [add(a, c), add(b, d), sub(a, c), sub(b, d)]


def dft8(x, sign):
    even, odd = dft4(x[0::2], sign), dft4(x[1::2], sign)
    r, i = odd[1]
    w1 = (HALF * (r - i), HALF * (i + r)) if sign > 0 else (HALF * (r + i), HALF * (i - r))
    w2 = turn(odd[2], sign)
    r, i = odd[3]
    w3 = (HALF * (-r - i), HALF * (r - i)) if sign > 0 else (HALF * (i - r), HALF * (-i - r))
    odd = [odd[0], w1, w2, w3]
    return [add(even[k], odd[k]) for k in range(4)] + [sub(even[k], odd[k]) for k in range(4)]


def twiddle(a, k, total, sign):
    if k % total == 0:
        return a
    c = math.cos(2.0 * math.pi * k / total)
    s = sign * math.sin(2.0 * math.pi * k / total)
    return (a[0] * c - a[1] * s, a[0] * s + a[1] * c)


def exponent(largest):
    return jnp.ceil(jnp.log2(jnp.maximum(largest, TINY))) + 1.0


def shrink(values):
    return values - jnp.clip(values, -THRESHOLD, THRESHOLD)


def product_kernel(*refs, packed, base, parts, stacked_rows):
    if packed:
        wr, wi, g_real, g_imag, g_exp, own_r, own_i, whole, z_out, sum_out = refs
        scale = jnp.exp2(g_exp[:, 0] - TOP)
        now_r = jnp.concatenate([g_real[d, 0] * scale[d] for d in range(parts)], axis=1)
        now_i = jnp.concatenate([g_imag[d, 0] * scale[d] for d in range(parts)], axis=1)
    else:
        wr, wi, g_real, g_imag, own_r, own_i, whole, z_out, sum_out = refs
        now_r = g_real[0]
        now_i = g_imag[0]
    f = base + pl.program_id(0)
    qr, qi = wr[f], wi[f]
    rows, n = now_r.shape
    if stacked_rows:
        p_r = whole[:, 0, 0].reshape(n, n)
        p_i = whole[:, 1, 0].reshape(n, n)
    else:
        p_r = whole[0, 0]
        p_i = whole[1, 0]
    left = jnp.concatenate([now_r, now_i], axis=0).astype(jnp.bfloat16)
    with_r = jnp.dot(left, p_r, preferred_element_type=jnp.float32)
    with_i = jnp.dot(left, p_i, preferred_element_type=jnp.float32)
    e_r = own_r[0].astype(jnp.float32) + (with_r[:rows] - with_i[rows:]) - (qr * now_r - qi * now_i)
    e_i = own_i[0].astype(jnp.float32) + (with_i[:rows] + with_r[rows:]) - (qr * now_i + qi * now_r)
    wide = n // parts
    squares = (e_r * e_r + e_i * e_i).reshape(rows // 8, 8, n).sum(axis=0)
    total = squares[:, :wide]
    for d in range(1, parts):
        total = total + squares[:, d * wide : (d + 1) * wide]
    sum_out[0] = total
    eb = jnp.concatenate([e_r, e_i], axis=0).astype(jnp.bfloat16)
    dims = (((1,), (1,)), ((), ()))
    back_r = lax.dot_general(eb, p_r, dims, preferred_element_type=jnp.float32)
    back_i = lax.dot_general(eb, p_i, dims, preferred_element_type=jnp.float32)
    h_r = qr * e_r + qi * e_i - (back_r[:rows] + back_i[rows:])
    h_i = qr * e_i - qi * e_r - (back_r[rows:] - back_i[:rows])
    z_r = now_r + STEP_LENGTH * h_r
    z_i = now_i + STEP_LENGTH * h_i
    blocks = rows // 8
    cut_r = [z_r[:, d * wide : (d + 1) * wide].reshape(blocks, 8, wide) for d in range(parts)]
    cut_i = [z_i[:, d * wide : (d + 1) * wide].reshape(blocks, 8, wide) for d in range(parts)]
    largest = jnp.maximum(jnp.abs(cut_r[0]), jnp.abs(cut_i[0]))
    for d in range(1, parts):
        largest = jnp.maximum(largest, jnp.maximum(jnp.abs(cut_r[d]), jnp.abs(cut_i[d])))
    power = exponent(largest.max(axis=0))
    factor = jnp.exp2(TOP - power)
    for d in range(parts):
        z_out[d, 0, :blocks] = cut_r[d] * factor[None]
        z_out[d, 0, blocks : 2 * blocks] = cut_i[d] * factor[None]
        z_out[d, 0, 2 * blocks] = power


def product(chunk, wave_r, wave_i, current, data_r, data_i, whole, parts):
    packed = not isinstance(current, tuple)
    count, rows, n = data_r.shape
    span = count // CHUNKS
    base = chunk * span
    wide = n // parts
    blocks = rows // 8
    stacked_rows = whole.ndim == 5
    smem = pl.BlockSpec(memory_space=pltpu.SMEM)
    own = pl.BlockSpec((1, rows, n), lambda f: (base + f, 0, 0))
    if packed:
        ins = [current, current, current]
        cur = [
            pl.BlockSpec((parts, 1, rows, wide), lambda f: (0, base + f, 0, 0)),
            pl.BlockSpec((parts, 1, rows, wide), lambda f: (0, count + base + f, 0, 0)),
            pl.BlockSpec((parts, 1, rows, wide), lambda f: (0, 2 * count, 0, 0)),
        ]
    else:
        ins = list(current)
        cur = [own, own]
    if stacked_rows:
        far = pl.BlockSpec((whole.shape[0], 2, 1, rows, n), lambda f: (0, 0, f, 0, 0))
    else:
        far = pl.BlockSpec((2, 1, n, n), lambda f: (0, f, 0, 0))
    kernel = partial(
        product_kernel, packed=packed, base=base, parts=parts, stacked_rows=stacked_rows
    )
    return pl.pallas_call(
        kernel,
        grid=(span,),
        in_specs=[smem, smem] + cur + [own, own, far],
        out_specs=[
            pl.BlockSpec((parts, 1, 2 * blocks + 1, 8, wide), lambda f: (0, f, 0, 0, 0)),
            pl.BlockSpec((1, 8, wide), lambda f: (f, 0, 0)),
        ],
        out_shape=[
            jax.ShapeDtypeStruct((parts, span, 2 * blocks + 1, 8, wide), jnp.float32),
            jax.ShapeDtypeStruct((span, 8, wide), jnp.float32),
        ],
        cost_estimate=pl.CostEstimate(
            flops=span * 16 * rows * n * n, bytes_accessed=span * 6 * n * n, transcendentals=0
        ),
        name=f"product_{chunk}_{int(packed)}",
    )(wave_r, wave_i, *ins, data_r, data_i, whole)


def transform_kernel(*refs, parts, count, span, group):
    ins, out, buf_r, buf_i = refs[:-3], refs[-3], refs[-2], refs[-1]
    total = parts * count
    norm = 1.0 / math.sqrt(total)

    def one(b, carry):
        def load(f):
            src, rest = divmod(f, count)
            chunk, j = divmod(rest, span)
            re, im, ex = ins[3 * chunk : 3 * chunk + 3]
            scale = jnp.exp2(ex[src, j, 0] - TOP) * norm
            return (re[src, j, b] * scale, im[src, j, b] * scale)

        for f0 in range(RADIX):
            got = dft8([load(RADIX * f1 + f0) for f1 in range(RADIX)], 1)
            for t1 in range(RADIX):
                v = twiddle(got[t1], f0 * t1, total, 1)
                buf_r[f0, t1], buf_i[f0, t1] = v
        largest = None
        for t1 in range(RADIX):
            z = dft8([(buf_r[f0, t1], buf_i[f0, t1]) for f0 in range(RADIX)], 1)
            x = [(shrink(r), shrink(i)) for r, i in z]
            for r, i in x:
                m = jnp.maximum(jnp.abs(r), jnp.abs(i))
                largest = m if largest is None else jnp.maximum(largest, m)
            got = dft8(x, -1)
            for f0 in range(RADIX):
                v = twiddle(got[f0], f0 * t1, total, -1)
                buf_r[f0, t1], buf_i[f0, t1] = v
        power = exponent(largest * (1.5 * math.sqrt(total)))
        factor = jnp.exp2(TOP - power) * norm
        at = pl.ds(pl.multiple_of(b * 8, 8), 8)
        for f0 in range(RADIX):
            got = dft8([(buf_r[f0, t1], buf_i[f0, t1]) for t1 in range(RADIX)], -1)
            for f1 in range(RADIX):
                dst, j = divmod(RADIX * f1 + f0, count)
                out[dst, j, at] = got[f1][0] * factor
                out[dst, count + j, at] = got[f1][1] * factor
        for dst in range(parts):
            out[dst, 2 * count, at] = power
        return carry

    lax.fori_loop(0, group, one, 0)


def transform(pieces, rows):
    parts, span, _, _, wide = pieces[0].shape
    count = span * CHUNKS
    blocks = rows // 8
    group = 2 if blocks % 2 == 0 else 1
    steps = blocks // group
    specs, ins = [], []
    for piece in pieces:
        ins += [piece] * 3
        specs += [
            pl.BlockSpec((parts, span, group, 8, wide), lambda g: (0, 0, g, 0, 0)),
            pl.BlockSpec((parts, span, group, 8, wide), lambda g: (0, 0, steps + g, 0, 0)),
            pl.BlockSpec((parts, span, 1, 8, wide), lambda g: (0, 0, 2 * blocks, 0, 0)),
        ]
    return pl.pallas_call(
        partial(transform_kernel, parts=parts, count=count, span=span, group=group),
        grid=(steps,),
        in_specs=specs,
        out_specs=pl.BlockSpec((parts, 2 * count + 1, 8 * group, wide), lambda g: (0, 0, g, 0)),
        out_shape=jax.ShapeDtypeStruct((parts, 2 * count + 1, rows, wide), jnp.float32),
        scratch_shapes=[pltpu.VMEM((RADIX, RADIX, 8, wide), jnp.float32)] * 2,
        name="transform",
    )(*ins)


def exchange(values):
    moved = lax.all_to_all(
        values.astype(jnp.float16), "af", split_axis=0, concat_axis=0, tiled=True
    )
    return moved.astype(jnp.float32)


def everywhere(values, sizes):
    total = sizes[0] * sizes[1]
    step = 1
    while step < total:
        pairs = [(i, i ^ step) for i in range(total)]
        values = values + lax.ppermute(values, ("af", "sa"), pairs)
        step *= 2
    return values


def on_device(data_r, data_i, wave_r, wave_i, primaries_r, primaries_i, *, sizes):
    parts, ring = sizes
    count, rows, n = data_r.shape
    total_f = count * parts
    span = count // CHUNKS
    wholes = []
    for c in range(CHUNKS):
        cut = slice(c * span, (c + 1) * span)
        mine = jnp.stack([data_r[cut], data_i[cut]])
        if rows % 16 == 0:
            wholes.append(lax.all_gather(mine, "sa"))
        else:
            wholes.append(lax.all_gather(mine, "sa", axis=2, tiled=True))
    current = (primaries_r, primaries_i)
    sums = []
    for _ in range(ITERS):
        pieces, partials = [], []
        for c in range(CHUNKS):
            z, s = product(c, wave_r, wave_i, current, data_r, data_i, wholes[c], parts)
            pieces.append(exchange(z))
            partials.append(s)
        sums.append(sum(jnp.sum(s) for s in partials))
        current = exchange(transform(pieces, rows))
    misfit = everywhere(jnp.stack(sums), sizes) / (total_f * n * n)
    scale = jnp.exp2(current[:, 2 * count] - TOP)[:, None]

    def whole_rows(part):
        return (part * scale).transpose(1, 2, 0, 3).reshape(count, rows, n)

    return whole_rows(current[:, :count]), whole_rows(current[:, count : 2 * count]), misfit


def solution(mesh):
    spec = P("af", "sa", None)
    sizes = (mesh.shape["af"], mesh.shape["sa"])
    return jax.shard_map(
        partial(on_device, sizes=sizes),
        mesh=mesh,
        in_specs=(spec, spec, P("af"), P("af"), spec, spec),
        out_specs=(spec, spec, P()),
        check_vma=False,
    )
```

time: 616 us -> 377 us (0.61); the launches traced: 607 us -> 375 us
  matrix products: 97.7 us -> 0 us
  local copies, waits for them, and re-layouts: 101 us -> 4.88 us
  waiting for transfers between devices: 247 us -> 173 us
  Pallas kernels: 0 us -> 64 us
  blocking collectives: 54.3 us -> 28.3 us
  other arithmetic: 56.9 us -> 45.9 us
  starting transfers between devices: 33.3 us -> 40 us
    dot_general x24 -> x0, matrix products: 97.7 us -> none  [the longest x16 52.7 us: highest(): jnp.dot(left, right, precision=lax.Precision.HIGHEST, preferred_element_t...]
    all_to_all x8 -> x9, waiting for transfers between devices: 88.6 us -> 9.12 us  [exchange(): lax.all_to_all(values.astype(jnp.float16), 'af', split_axis=0, concat_axi...]
    pallas_call x0 -> x10, Pallas kernels: none -> 64 us  [the longest x8 49.7 us: product(): pl.pallas_call(kernel, grid=(span,), in_specs=[smem, smem] + cur + [own,...]
    psum x1 -> x0, blocking collectives: 54.3 us -> none  [on_device(): totals = lax.psum(jnp.stack(local_sums), ('af', 'sa'))]
    unnamed x90 -> x16, local copies, waits for them, and re-layouts: 51.7 us -> 0.03 us
    all_to_all x4 -> x0, other arithmetic: 30.5 us -> none  [the longest x2 15.2 us: on_device(): lax.all_to_all(stepped_real, 'af', split_axis=2, concat_axis=0, tiled=True)]
    all_to_all x11 -> x0, local copies, waits for them, and re-layouts: 29.6 us -> none  [the longest x3 9.29 us: on_device(): lax.all_to_all(freq_real, 'af', split_axis=0, concat_axis=2, tiled=True)]
    all_to_all x0 -> x1, blocking collectives: none -> 28.3 us  [exchange(): lax.all_to_all(values.astype(jnp.float16), 'af', split_axis=0, concat_axi...]
  transfers between devices with their start and end apart: 10 -> 18, of which waited for: 9 -> 11; matrix products, arithmetic and copies ran while one was open for 16% -> 8% of each run, Pallas kernels for 0% -> 12%
where the time goes in v1:
time: 377 us; the launch traced here: 375 us
  waiting for transfers between devices  173 us (46%)
  Pallas kernels  64 us (17%)
  other arithmetic  45.9 us (12%)
  starting transfers between devices  40 us (11%)
  blocking collectives  28.3 us (8%)
  between operations  19.1 us (5%)
  local copies, waits for them, and re-layouts  4.88 us (1%)
    all_gather x4, waiting for transfers between devices, on_device(): wholes.append(lax.all_gather(mine, 'sa'))  153 us
    pallas_call x8, Pallas kernels, product(): pl.pallas_call(kernel, grid=(span,), in_specs=[smem, smem] + cur + [own,...  49.7 us
    all_to_all x9, starting transfers between devices, exchange(): lax.all_to_all(values.astype(jnp.float16), 'af', split_axis=0, concat_axi...  34.4 us
    all_to_all x1, blocking collectives, exchange(): lax.all_to_all(values.astype(jnp.float16), 'af', split_axis=0, concat_axi...  28.3 us
    convert_element_type x10, other arithmetic, exchange(): values.astype(jnp.float16)  24.3 us
    pallas_call x2, Pallas kernels, transform(): pl.pallas_call(partial(transform_kernel, parts=parts, count=count, span=s...  14.3 us
    convert_element_type x10, other arithmetic, exchange(): return moved.astype(jnp.float32)  11.7 us
    ppermute x5, waiting for transfers between devices, everywhere(): values = values + lax.ppermute(values, ('af', 'sa'), pairs)  10.9 us
  transfers between devices with their start and end apart: 18, of which 11 were waited for; matrix products, arithmetic and copies ran while one was open for 8% of the time, Pallas kernels for 12%

profile of v1, /device:TPU:0, one launch (start us, length us, event | category | flops | bytes accessed | tf_op | source)
XLA Modules:
  0.0 375.1 jit_solution(10173105278828183066)
XLA Ops:
  7.2 1.7 slice_bitcast_fusion
  12.5 47.2 %all-gather.9.cloned.1.call-done = bf16[16,4,64,512]{3,2,1,0:T(8,128)(2,1)} async-done(((bf16[2,4,64,512]{3,2,1,0:T(8,128)(2,1)}), bf16[16,4,64,512]{3,2,1,0:T(8,128)(2,1)}) %all-gather.9.cloned.1.call-update) | async-done | bytes 4194320 | tf_op jit(solution)/shard_map/all_gather | solution.py:261
  59.8 6.2 %product_0_0.1 = (f32[4,4,17,8,128]{4,3,2,1,0:T(8,128)}, f32[4,8,128]{2,1,0:T(8,128)}) custom-call(f32[16]{0:T(128)} %refs_0_.15, f32[16]{0:T(128)} %refs_1_.15, f32[16,64,512]{2,1,0:T(8,128)} %refs_2_.7, f32[16,64,512]{2,1,0:T(8,128)} %refs_3_.7, bf16[16,64,512]{2,1,0:T(8,128)(2,1)} %refs_5_.15, bf16[16,64,512]{2,1,0:T(8,128)(2,1)} %refs_6_.7, ...), custom_call_target="tpu_custom_call" | custom-call | flops 1073741824 | bytes 6291456 | tf_op jit(solution)/shard_map/product_0_0/pallas_call | solution.py:145
  66.0 2.2 convert_element_type.60
  68.1 3.6 all-to-all-start
  71.8 35.3 %all-gather.11.cloned.1.call-done = bf16[16,4,64,512]{3,2,1,0:T(8,128)(2,1)} async-done(((bf16[2,4,64,512]{3,2,1,0:T(8,128)(2,1)}), bf16[16,4,64,512]{3,2,1,0:T(8,128)(2,1)}) %all-gather.11.cloned.1.call-update) | async-done | bytes 4194320 | tf_op jit(solution)/shard_map/all_gather | solution.py:261
  107.1 6.2 %product_1_0.1 = (f32[4,4,17,8,128]{4,3,2,1,0:T(8,128)}, f32[4,8,128]{2,1,0:T(8,128)}) custom-call(f32[16]{0:T(128)} %refs_0_.15, f32[16]{0:T(128)} %refs_1_.15, f32[16,64,512]{2,1,0:T(8,128)} %refs_2_.7, f32[16,64,512]{2,1,0:T(8,128)} %refs_3_.7, bf16[16,64,512]{2,1,0:T(8,128)(2,1)} %refs_5_.15, bf16[16,64,512]{2,1,0:T(8,128)(2,1)} %refs_6_.7, ...), custom_call_target="tpu_custom_call" | custom-call | flops 1073741824 | bytes 6291456 | tf_op jit(solution)/shard_map/product_1_0/pallas_call | solution.py:145
  113.3 2.2 convert_element_type.62
  115.5 3.7 all-to-all-start.1
  119.1 35.3 %all-gather.13.cloned.1.call-done = bf16[16,4,64,512]{3,2,1,0:T(8,128)(2,1)} async-done(((bf16[2,4,64,512]{3,2,1,0:T(8,128)(2,1)}), bf16[16,4,64,512]{3,2,1,0:T(8,128)(2,1)}) %all-gather.13.cloned.1.call-update) | async-done | bytes 4194320 | tf_op jit(solution)/shard_map/all_gather | solution.py:261
  154.4 6.2 %product_2_0.1 = (f32[4,4,17,8,128]{4,3,2,1,0:T(8,128)}, f32[4,8,128]{2,1,0:T(8,128)}) custom-call(f32[16]{0:T(128)} %refs_0_.15, f32[16]{0:T(128)} %refs_1_.15, f32[16,64,512]{2,1,0:T(8,128)} %refs_2_.7, f32[16,64,512]{2,1,0:T(8,128)} %refs_3_.7, bf16[16,64,512]{2,1,0:T(8,128)(2,1)} %refs_5_.15, bf16[16,64,512]{2,1,0:T(8,128)(2,1)} %refs_6_.7, ...), custom_call_target="tpu_custom_call" | custom-call | flops 1073741824 | bytes 6291456 | tf_op jit(solution)/shard_map/product_2_0/pallas_call | solution.py:145
  160.6 2.2 convert_element_type.64
  162.8 3.7 all-to-all-start.2
  166.4 35.1 %all-gather.15.cloned.1.call-done = bf16[16,4,64,512]{3,2,1,0:T(8,128)(2,1)} async-done(((bf16[2,4,64,512]{3,2,1,0:T(8,128)(2,1)}), bf16[16,4,64,512]{3,2,1,0:T(8,128)(2,1)}) %all-gather.15.cloned.1.call-update) | async-done | bytes 4194320 | tf_op jit(solution)/shard_map/all_gather | solution.py:261
  201.6 6.2 %product_3_0.1 = (f32[4,4,17,8,128]{4,3,2,1,0:T(8,128)}, f32[4,8,128]{2,1,0:T(8,128)}) custom-call(f32[16]{0:T(128)} %refs_0_.15, f32[16]{0:T(128)} %refs_1_.15, f32[16,64,512]{2,1,0:T(8,128)} %refs_2_.7, f32[16,64,512]{2,1,0:T(8,128)} %refs_3_.7, bf16[16,64,512]{2,1,0:T(8,128)(2,1)} %refs_5_.15, bf16[16,64,512]{2,1,0:T(8,128)(2,1)} %refs_6_.7, ...), custom_call_target="tpu_custom_call" | custom-call | flops 1073741824 | bytes 6291456 | tf_op jit(solution)/shard_map/product_3_0/pallas_call | solution.py:145
  207.7 2.1 convert_element_type.66
  209.9 3.6 all-to-all-start.3
  216.8 5.6 %all-to-all-done.3 = f16[4,4,17,8,128]{4,3,2,1,0:T(8,128)(2,1)S(1)} async-done(((f16[4,4,17,8,128]{4,3,2,1,0:T(8,128)(2,1)}), f16[4,4,17,8,128]{4,3,2,1,0:T(8,128)(2,1)S(1)}, u32[]{:S(2)}, u32[]{:S(2)}) %all-to-all-start.3) | async-done | bytes 557088 | tf_op jit(solution)/shard_map/all_to_all | solution.py:235
  223.5 7.2 %transform.2 = f32[4,33,64,128]{3,2,1,0:T(8,128)} custom-call(f32[4,4,17,8,128]{4,3,2,1,0:T(8,128)} %convert_element_type.61.refs_0_.refs_1_.refs_2_, f32[4,4,17,8,128]{4,3,2,1,0:T(8,128)} %convert_element_type.61.refs_0_.refs_1_.refs_2_, f32[4,4,17,8,128]{4,3,2,1,0:T(8,128)} %convert_element_type.61.refs_0_.refs_1_.refs_2_, ...), custom_call_target="tpu_custom_call" | custom-call | tf_op jit(solution)/shard_map/transform/pallas_call | solution.py:223
  230.6 2.8 convert_element_type.68
  233.4 28.3 %all_to_all.50 = f16[4,33,64,128]{3,2,1,0:T(8,128)(2,1)S(1)} all-to-all(f16[4,33,64,128]{3,2,1,0:T(8,128)(2,1)S(1)} %convert_element_type.68), channel_id=1, replica_groups=mesh['af'=4,'sa'=8] {'af'}, dimensions={0} | all-to-all | bytes 4325376 | tf_op jit(solution)/shard_map/all_to_all | solution.py:235
  261.7 2.5 convert_element_type.69.refs_2_.refs_3_.refs_4_
  264.3 6.2 %product_2_1.1 = (f32[4,4,17,8,128]{4,3,2,1,0:T(8,128)}, f32[4,8,128]{2,1,0:T(8,128)}) custom-call(f32[16]{0:T(128)} %refs_0_.15, f32[16]{0:T(128)} %refs_1_.15, f32[4,33,64,128]{3,2,1,0:T(8,128)} %convert_element_type.69.refs_2_.refs_3_.refs_4_, f32[4,33,64,128]{3,2,1,0:T(8,128)} %convert_element_type.69.refs_2_.refs_3_.refs_4_, ...), custom_call_target="tpu_custom_call" | custom-call | flops 1073741824 | bytes 6291456 | tf_op jit(solution)/shard_map/product_2_1/pallas_call | solution.py:145
  270.5 2.1 convert_element_type.74
  272.6 3.5 all-to-all-start.7
  276.1 6.3 %product_1_1.1 = (f32[4,4,17,8,128]{4,3,2,1,0:T(8,128)}, f32[4,8,128]{2,1,0:T(8,128)}) custom-call(f32[16]{0:T(128)} %refs_0_.15, f32[16]{0:T(128)} %refs_1_.15, f32[4,33,64,128]{3,2,1,0:T(8,128)} %convert_element_type.69.refs_2_.refs_3_.refs_4_, f32[4,33,64,128]{3,2,1,0:T(8,128)} %convert_element_type.69.refs_2_.refs_3_.refs_4_, ...), custom_call_target="tpu_custom_call" | custom-call | flops 1073741824 | bytes 6291456 | tf_op jit(solution)/shard_map/product_1_1/pallas_call | solution.py:145
  282.4 2.2 convert_element_type.72
  284.5 4.1 %all-to-all-start.6 = ((f16[4,4,17,8,128]{4,3,2,1,0:T(8,128)(2,1)}), f16[4,4,17,8,128]{4,3,2,1,0:T(8,128)(2,1)S(1)}, u32[]{:S(2)}, u32[]{:S(2)}) async-start(f16[4,4,17,8,128]{4,3,2,1,0:T(8,128)(2,1)} %convert_element_type.72), calls=%async_computation.6 | async-start | bytes 1114112 | tf_op jit(solution)/shard_map/all_to_all | solution.py:235
  288.7 6.2 %product_0_1.1 = (f32[4,4,17,8,128]{4,3,2,1,0:T(8,128)}, f32[4,8,128]{2,1,0:T(8,128)}) custom-call(f32[16]{0:T(128)} %refs_0_.15, f32[16]{0:T(128)} %refs_1_.15, f32[4,33,64,128]{3,2,1,0:T(8,128)} %convert_element_type.69.refs_2_.refs_3_.refs_4_, f32[4,33,64,128]{3,2,1,0:T(8,128)} %convert_element_type.69.refs_2_.refs_3_.refs_4_, ...), custom_call_target="tpu_custom_call" | custom-call | flops 1073741824 | bytes 6291456 | tf_op jit(solution)/shard_map/product_0_1/pallas_call | solution.py:145
  294.9 2.1 convert_element_type.70
  297.0 4.2 %all-to-all-start.5 = ((f16[4,4,17,8,128]{4,3,2,1,0:T(8,128)(2,1)}), f16[4,4,17,8,128]{4,3,2,1,0:T(8,128)(2,1)S(1)}, u32[]{:S(2)}, u32[]{:S(2)}) async-start(f16[4,4,17,8,128]{4,3,2,1,0:T(8,128)(2,1)} %convert_element_type.70), calls=%async_computation.5 | async-start | bytes 1114112 | tf_op jit(solution)/shard_map/all_to_all | solution.py:235
  301.2 6.2 %product_3_1.1 = (f32[4,4,17,8,128]{4,3,2,1,0:T(8,128)}, f32[4,8,128]{2,1,0:T(8,128)}) custom-call(f32[16]{0:T(128)} %refs_0_.15, f32[16]{0:T(128)} %refs_1_.15, f32[4,33,64,128]{3,2,1,0:T(8,128)} %convert_element_type.69.refs_2_.refs_3_.refs_4_, f32[4,33,64,128]{3,2,1,0:T(8,128)} %convert_element_type.69.refs_2_.refs_3_.refs_4_, ...), custom_call_target="tpu_custom_call" | custom-call | flops 1073741824 | bytes 6291456 | tf_op jit(solution)/shard_map/product_3_1/pallas_call | solution.py:145
  307.4 2.1 convert_element_type.76
  309.6 4.2 %all-to-all-start.8 = ((f16[4,4,17,8,128]{4,3,2,1,0:T(8,128)(2,1)}), f16[4,4,17,8,128]{4,3,2,1,0:T(8,128)(2,1)S(1)}, u32[]{:S(2)}, u32[]{:S(2)}) async-start(f16[4,4,17,8,128]{4,3,2,1,0:T(8,128)(2,1)} %convert_element_type.76), calls=%async_computation.8 | async-start | bytes 1114112 | tf_op jit(solution)/shard_map/all_to_all | solution.py:235
  317.0 3.5 all-to-all-done.8
  321.6 7.2 %transform.3 = f32[4,33,64,128]{3,2,1,0:T(8,128)} custom-call(f32[4,4,17,8,128]{4,3,2,1,0:T(8,128)} %convert_element_type.71.refs_0_.refs_1_.refs_2_, f32[4,4,17,8,128]{4,3,2,1,0:T(8,128)} %convert_element_type.71.refs_0_.refs_1_.refs_2_, f32[4,4,17,8,128]{4,3,2,1,0:T(8,128)} %convert_element_type.71.refs_0_.refs_1_.refs_2_, ...), custom_call_target="tpu_custom_call" | custom-call | tf_op jit(solution)/shard_map/transform/pallas_call | solution.py:223
  328.8 4.2 %convert_element_type.78 = f16[4,33,64,128]{3,2,1,0:T(8,128)(2,1)} convert(f32[4,33,64,128]{3,2,1,0:T(8,128)} %transform.3) | non-fusion elementwise | flops 1081344 | bytes 6488064 | tf_op jit(solution)/shard_map/convert_element_type | solution.py:236
  333.1 3.8 %all-to-all-start.9 = ((f16[4,33,64,128]{3,2,1,0:T(8,128)(2,1)}), f16[4,33,64,128]{3,2,1,0:T(8,128)(2,1)S(1)}, u32[]{:S(2)}, u32[]{:S(2)}) async-start(f16[4,33,64,128]{3,2,1,0:T(8,128)(2,1)} %convert_element_type.78), calls=%async_computation.9 | async-start | bytes 4325376 | tf_op jit(solution)/shard_map/all_to_all | solution.py:235
  347.0 1.1 collective-permute-done
  348.5 3.3 collective-permute-done.1
  351.8 1.2 collective-permute-start.2
  353.1 3.2 collective-permute-done.2
  356.3 2.0 collective-permute-start.3
  358.3 1.6 collective-permute-done.3
  359.9 2.0 collective-permute-start.4
  361.9 1.6 collective-permute-done.4
  365.4 1.6 copy.17
  367.0 1.6 copy.18
  (62 shorter events, 19.7 us)
Async XLA Ops:
  7.2 52.6 %all-gather.9.cloned.1.call-start = ((), (), s32[]{:S(2)}) async-start(), calls=%async_computation.10 | async-start | bytes 4718592 | tf_op jit(solution)/shard_map/all_gather | solution.py:261
  9.7 97.3 %all-gather.11.cloned.1.call-start = ((), (), s32[]{:S(2)}) async-start(), calls=%async_computation.11 | async-start | bytes 4718592 | tf_op jit(solution)/shard_map/all_gather | solution.py:261
  10.7 143.7 %all-gather.13.cloned.1.call-start = ((), (), s32[]{:S(2)}) async-start(), calls=%async_computation.12 | async-start | bytes 4718592 | tf_op jit(solution)/shard_map/all_gather | solution.py:261
  11.6 189.9 %all-gather.15.cloned.1.call-start = ((), (), s32[]{:S(2)}) async-start(), calls=%async_computation.13 | async-start | bytes 4718592 | tf_op jit(solution)/shard_map/all_gather | solution.py:261
  68.1 47.3 %all-to-all-start = ((f16[4,4,17,8,128]{4,3,2,1,0:T(8,128)(2,1)}), f16[4,4,17,8,128]{4,3,2,1,0:T(8,128)(2,1)S(1)}, u32[]{:S(2)}, u32[]{:S(2)}) async-start(f16[4,4,17,8,128]{4,3,2,1,0:T(8,128)(2,1)} %convert_element_type.60), calls=%async_computation | async-start | bytes 1114112 | tf_op jit(solution)/shard_map/all_to_all | solution.py:235
  115.5 47.3 %all-to-all-start.1 = ((f16[4,4,17,8,128]{4,3,2,1,0:T(8,128)(2,1)}), f16[4,4,17,8,128]{4,3,2,1,0:T(8,128)(2,1)S(1)}, u32[]{:S(2)}, u32[]{:S(2)}) async-start(f16[4,4,17,8,128]{4,3,2,1,0:T(8,128)(2,1)} %convert_element_type.62), calls=%async_computation.1 | async-start | bytes 1114112 | tf_op jit(solution)/shard_map/all_to_all | solution.py:235
  162.8 47.1 %all-to-all-start.2 = ((f16[4,4,17,8,128]{4,3,2,1,0:T(8,128)(2,1)}), f16[4,4,17,8,128]{4,3,2,1,0:T(8,128)(2,1)S(1)}, u32[]{:S(2)}, u32[]{:S(2)}) async-start(f16[4,4,17,8,128]{4,3,2,1,0:T(8,128)(2,1)} %convert_element_type.64), calls=%async_computation.2 | async-start | bytes 1114112 | tf_op jit(solution)/shard_map/all_to_all | solution.py:235
  209.9 12.5 %all-to-all-start.3 = ((f16[4,4,17,8,128]{4,3,2,1,0:T(8,128)(2,1)}), f16[4,4,17,8,128]{4,3,2,1,0:T(8,128)(2,1)S(1)}, u32[]{:S(2)}, u32[]{:S(2)}) async-start(f16[4,4,17,8,128]{4,3,2,1,0:T(8,128)(2,1)} %convert_element_type.66), calls=%async_computation.3 | async-start | bytes 1114112 | tf_op jit(solution)/shard_map/all_to_all | solution.py:235
  272.6 11.9 %all-to-all-start.7 = ((f16[4,4,17,8,128]{4,3,2,1,0:T(8,128)(2,1)}), f16[4,4,17,8,128]{4,3,2,1,0:T(8,128)(2,1)S(1)}, u32[]{:S(2)}, u32[]{:S(2)}) async-start(f16[4,4,17,8,128]{4,3,2,1,0:T(8,128)(2,1)} %convert_element_type.74), calls=%async_computation.7 | async-start | bytes 1114112 | tf_op jit(solution)/shard_map/all_to_all | solution.py:235
  284.5 12.5 %all-to-all-start.6 = ((f16[4,4,17,8,128]{4,3,2,1,0:T(8,128)(2,1)}), f16[4,4,17,8,128]{4,3,2,1,0:T(8,128)(2,1)S(1)}, u32[]{:S(2)}, u32[]{:S(2)}) async-start(f16[4,4,17,8,128]{4,3,2,1,0:T(8,128)(2,1)} %convert_element_type.72), calls=%async_computation.6 | async-start | bytes 1114112 | tf_op jit(solution)/shard_map/all_to_all | solution.py:235
  297.0 12.6 %all-to-all-start.5 = ((f16[4,4,17,8,128]{4,3,2,1,0:T(8,128)(2,1)}), f16[4,4,17,8,128]{4,3,2,1,0:T(8,128)(2,1)S(1)}, u32[]{:S(2)}, u32[]{:S(2)}) async-start(f16[4,4,17,8,128]{4,3,2,1,0:T(8,128)(2,1)} %convert_element_type.70), calls=%async_computation.5 | async-start | bytes 1114112 | tf_op jit(solution)/shard_map/all_to_all | solution.py:235
  309.6 10.9 %all-to-all-start.8 = ((f16[4,4,17,8,128]{4,3,2,1,0:T(8,128)(2,1)}), f16[4,4,17,8,128]{4,3,2,1,0:T(8,128)(2,1)S(1)}, u32[]{:S(2)}, u32[]{:S(2)}) async-start(f16[4,4,17,8,128]{4,3,2,1,0:T(8,128)(2,1)} %convert_element_type.76), calls=%async_computation.8 | async-start | bytes 1114112 | tf_op jit(solution)/shard_map/all_to_all | solution.py:235
  333.0 3.8 %copy-start = (f32[4,8,128]{2,1,0:T(8,128)S(1)}, f32[4,8,128]{2,1,0:T(8,128)}, u32[]{:S(2)}) copy-start(f32[4,8,128]{2,1,0:T(8,128)} %get-tuple-element.27) | copy-start | bytes 49156
  333.0 4.4 %copy-start.1 = (f32[4,8,128]{2,1,0:T(8,128)S(1)}, f32[4,8,128]{2,1,0:T(8,128)}, u32[]{:S(2)}) copy-start(f32[4,8,128]{2,1,0:T(8,128)} %get-tuple-element.28) | copy-start | bytes 49156
  333.0 5.0 %copy-start.2 = (f32[4,8,128]{2,1,0:T(8,128)S(1)}, f32[4,8,128]{2,1,0:T(8,128)}, u32[]{:S(2)}) copy-start(f32[4,8,128]{2,1,0:T(8,128)} %get-tuple-element.29) | copy-start | bytes 49156
  333.0 5.6 %copy-start.3 = (f32[4,8,128]{2,1,0:T(8,128)S(1)}, f32[4,8,128]{2,1,0:T(8,128)}, u32[]{:S(2)}) copy-start(f32[4,8,128]{2,1,0:T(8,128)} %get-tuple-element.30) | copy-start | bytes 49156
  333.0 8.8 %copy-start.6 = (f32[4,8,128]{2,1,0:T(8,128)S(1)}, f32[4,8,128]{2,1,0:T(8,128)}, u32[]{:S(2)}) copy-start(f32[4,8,128]{2,1,0:T(8,128)} %get-tuple-element.31) | copy-start | bytes 49156
  333.0 9.4 %copy-start.5 = (f32[4,8,128]{2,1,0:T(8,128)S(1)}, f32[4,8,128]{2,1,0:T(8,128)}, u32[]{:S(2)}) copy-start(f32[4,8,128]{2,1,0:T(8,128)} %get-tuple-element.32) | copy-start | bytes 49156
  333.0 10.0 %copy-start.4 = (f32[4,8,128]{2,1,0:T(8,128)S(1)}, f32[4,8,128]{2,1,0:T(8,128)}, u32[]{:S(2)}) copy-start(f32[4,8,128]{2,1,0:T(8,128)} %get-tuple-element.33) | copy-start | bytes 49156
  333.0 10.6 %copy-start.7 = (f32[4,8,128]{2,1,0:T(8,128)S(1)}, f32[4,8,128]{2,1,0:T(8,128)}, u32[]{:S(2)}) copy-start(f32[4,8,128]{2,1,0:T(8,128)} %get-tuple-element.34) | copy-start | bytes 49156
  333.1 30.9 %all-to-all-start.9 = ((f16[4,33,64,128]{3,2,1,0:T(8,128)(2,1)}), f16[4,33,64,128]{3,2,1,0:T(8,128)(2,1)S(1)}, u32[]{:S(2)}, u32[]{:S(2)}) async-start(f16[4,33,64,128]{3,2,1,0:T(8,128)(2,1)} %convert_element_type.78), calls=%async_computation.9 | async-start | bytes 4325376 | tf_op jit(solution)/shard_map/all_to_all | solution.py:235
  347.0 1.2 collective-permute-start
  348.2 3.6 collective-permute-start.1
  351.8 4.5 %collective-permute-start.2 = (f32[2]{0:T(128)S(1)}, f32[2]{0:T(128)S(1)}, u32[]{:S(2)}, u32[]{:S(2)}) collective-permute-start(f32[2]{0:T(128)S(1)} %fusion.6), channel_id=1, source_target_pairs={{0,4},{1,5},{2,6},{3,7},{4,0},{5,1},{6,2},{7,3},{8,12},{9,13},{10,... | collective-permute-start | bytes 32 | tf_op jit(solution)/shard_map/ppermute | solution.py:246
  356.3 3.6 collective-permute-start.3
  359.9 3.6 collective-permute-start.4
Sparse Core Ops, SparseCore 0:
  10.1 49.5 all-gather.8
  61.4 45.6 all-gather.10
  108.7 45.6 all-gather.12
  155.8 45.6 all-gather.14

commit v2 on v1

--- a/solution.py
+++ b/solution.py
@@ -12,6 +12,8 @@
 STEP_LENGTH = 0.02
 THRESHOLD = 0.25
 CHUNKS = 4
+MOST_RING = 8
+GROUPS = 2
 TOP = 15.0
 TINY = 1e-30
 RADIX = 8
@@ -63,20 +65,40 @@
     return values - jnp.clip(values, -THRESHOLD, THRESHOLD)
 
 
-def product_kernel(*refs, packed, base, parts, stacked_rows):
+def gathered(slots, slot_ranks, p_scr):
+    rows = slots[0].shape[2]
+    for d, ref in enumerate(slots):
+        at = pl.ds(pl.multiple_of(slot_ranks[d] * rows, rows), rows)
+        p_scr[0, at] = ref[0, 0]
+        p_scr[1, at] = ref[1, 0]
+    return p_scr[0], p_scr[1]
+
+
+def product_kernel(*refs, packed, parts, base, stacked_rows, slots):
+    if slots:
+        p_scr = refs[-1]
+        z_out, sum_out = refs[-3:-1]
+        ranks, whole = refs[-4 - slots], refs[-3 - slots : -3]
+        refs = refs[: -4 - slots]
+    else:
+        z_out, sum_out = refs[-2:]
+        whole = refs[-3]
+        refs = refs[:-3]
     if packed:
-        wr, wi, g_real, g_imag, g_exp, own_r, own_i, whole, z_out, sum_out = refs
+        wr, wi, g_real, g_imag, g_exp, own_r, own_i = refs
         scale = jnp.exp2(g_exp[:, 0] - TOP)
         now_r = jnp.concatenate([g_real[d, 0] * scale[d] for d in range(parts)], axis=1)
         now_i = jnp.concatenate([g_imag[d, 0] * scale[d] for d in range(parts)], axis=1)
     else:
-        wr, wi, g_real, g_imag, own_r, own_i, whole, z_out, sum_out = refs
+        wr, wi, g_real, g_imag, own_r, own_i = refs
         now_r = g_real[0]
         now_i = g_imag[0]
     f = base + pl.program_id(0)
     qr, qi = wr[f], wi[f]
     rows, n = now_r.shape
-    if stacked_rows:
+    if slots:
+        p_r, p_i = gathered(whole, ranks, p_scr)
+    elif stacked_rows:
         p_r = whole[:, 0, 0].reshape(n, n)
         p_i = whole[:, 1, 0].reshape(n, n)
     else:
@@ -115,37 +137,53 @@
         z_out[d, 0, 2 * blocks] = power
 
 
-def product(chunk, wave_r, wave_i, current, data_r, data_i, whole, parts):
+def product(chunk, wave_r, wave_i, current, data_r, data_i, whole, parts, ranks):
     packed = not isinstance(current, tuple)
     count, rows, n = data_r.shape
     span = count // CHUNKS
     base = chunk * span
     wide = n // parts
     blocks = rows // 8
-    stacked_rows = whole.ndim == 5
+    slots = len(whole) if isinstance(whole, list) else 0
+    stacked_rows = not slots and whole.ndim == 5
     smem = pl.BlockSpec(memory_space=pltpu.SMEM)
     own = pl.BlockSpec((1, rows, n), lambda f: (base + f, 0, 0))
     if packed:
         ins = [current, current, current]
+        held = current.shape[1] // 2
+        first = base % held
         cur = [
-            pl.BlockSpec((parts, 1, rows, wide), lambda f: (0, base + f, 0, 0)),
-            pl.BlockSpec((parts, 1, rows, wide), lambda f: (0, count + base + f, 0, 0)),
-            pl.BlockSpec((parts, 1, rows, wide), lambda f: (0, 2 * count, 0, 0)),
+            pl.BlockSpec((parts, 1, rows, wide), lambda f: (0, first + f, 0, 0)),
+            pl.BlockSpec((parts, 1, rows, wide), lambda f: (0, held + first + f, 0, 0)),
+            pl.BlockSpec((parts, 1, rows, wide), lambda f: (0, 2 * held, 0, 0)),
         ]
     else:
         ins = list(current)
         cur = [own, own]
-    if stacked_rows:
-        far = pl.BlockSpec((whole.shape[0], 2, 1, rows, n), lambda f: (0, 0, f, 0, 0))
-    else:
-        far = pl.BlockSpec((2, 1, n, n), lambda f: (0, f, 0, 0))
+    scratch = []
+    if slots:
+        far = [smem] + [pl.BlockSpec((2, 1, rows, n), lambda f: (0, f, 0, 0))] * slots
+        tail = [ranks] + whole
+        scratch = [pltpu.VMEM((2, n, n), jnp.bfloat16)]
+    elif stacked_rows:
+        far = [pl.BlockSpec((whole.shape[0], 2, 1, rows, n), lambda f: (0, 0, f, 0, 0))]
+        tail = [whole]
+    else:
+        far = [pl.BlockSpec((2, 1, n, n), lambda f: (0, f, 0, 0))]
+        tail = [whole]
     kernel = partial(
-        product_kernel, packed=packed, base=base, parts=parts, stacked_rows=stacked_rows
+        product_kernel,
+        packed=packed,
+        base=base,
+        parts=parts,
+        stacked_rows=stacked_rows,
+        slots=slots,
     )
     return pl.pallas_call(
         kernel,
         grid=(span,),
-        in_specs=[smem, smem] + cur + [own, own, far],
+        in_specs=[smem, smem] + cur + [own, own] + far,
+        scratch_shapes=scratch,
         out_specs=[
             pl.BlockSpec((parts, 1, 2 * blocks + 1, 8, wide), lambda f: (0, f, 0, 0, 0)),
             pl.BlockSpec((1, 8, wide), lambda f: (f, 0, 0)),
@@ -158,11 +196,12 @@
             flops=span * 16 * rows * n * n, bytes_accessed=span * 6 * n * n, transcendentals=0
         ),
         name=f"product_{chunk}_{int(packed)}",
-    )(wave_r, wave_i, *ins, data_r, data_i, whole)
-
-
-def transform_kernel(*refs, parts, count, span, group):
-    ins, out, buf_r, buf_i = refs[:-3], refs[-3], refs[-2], refs[-1]
+    )(wave_r, wave_i, *ins, data_r, data_i, *tail)
+
+
+def transform_kernel(*refs, parts, count, span, group, held):
+    ins, outs = refs[: 3 * CHUNKS], refs[3 * CHUNKS : -2]
+    buf_r, buf_i = refs[-2:]
     total = parts * count
     norm = 1.0 / math.sqrt(total)
 
@@ -196,22 +235,25 @@
         for f0 in range(RADIX):
             got = dft8([(buf_r[f0, t1], buf_i[f0, t1]) for t1 in range(RADIX)], -1)
             for f1 in range(RADIX):
-                dst, j = divmod(RADIX * f1 + f0, count)
-                out[dst, j, at] = got[f1][0] * factor
-                out[dst, count + j, at] = got[f1][1] * factor
+                dst, rest = divmod(RADIX * f1 + f0, count)
+                which, j = divmod(rest, held)
+                outs[which][dst, j, at] = got[f1][0] * factor
+                outs[which][dst, held + j, at] = got[f1][1] * factor
         for dst in range(parts):
-            out[dst, 2 * count, at] = power
+            for out in outs:
+                out[dst, 2 * held, at] = power
         return carry
 
     lax.fori_loop(0, group, one, 0)
 
 
-def transform(pieces, rows):
+def transform(pieces, rows, groups):
     parts, span, _, _, wide = pieces[0].shape
     count = span * CHUNKS
     blocks = rows // 8
     group = 2 if blocks % 2 == 0 else 1
     steps = blocks // group
+    held = count // groups
     specs, ins = [], []
     for piece in pieces:
         ins += [piece] * 3
@@ -221,63 +263,125 @@
             pl.BlockSpec((parts, span, 1, 8, wide), lambda g: (0, 0, 2 * blocks, 0, 0)),
         ]
     return pl.pallas_call(
-        partial(transform_kernel, parts=parts, count=count, span=span, group=group),
+        partial(
+            transform_kernel, parts=parts, count=count, span=span, group=group, held=held
+        ),
         grid=(steps,),
         in_specs=specs,
-        out_specs=pl.BlockSpec((parts, 2 * count + 1, 8 * group, wide), lambda g: (0, 0, g, 0)),
-        out_shape=jax.ShapeDtypeStruct((parts, 2 * count + 1, rows, wide), jnp.float32),
+        out_specs=[pl.BlockSpec((parts, 2 * held + 1, 8 * group, wide), lambda g: (0, 0, g, 0))]
+        * groups,
+        out_shape=[jax.ShapeDtypeStruct((parts, 2 * held + 1, rows, wide), jnp.float32)] * groups,
         scratch_shapes=[pltpu.VMEM((RADIX, RADIX, 8, wide), jnp.float32)] * 2,
         name="transform",
     )(*ins)
 
 
-def exchange(values):
-    moved = lax.all_to_all(
+def after(value, *others):
+    return lax.optimization_barrier((value, *others))[0]
+
+
+def send(values):
+    return lax.all_to_all(
         values.astype(jnp.float16), "af", split_axis=0, concat_axis=0, tiled=True
     )
-    return moved.astype(jnp.float32)
-
-
-def everywhere(values, sizes):
-    total = sizes[0] * sizes[1]
-    step = 1
-    while step < total:
-        pairs = [(i, i ^ step) for i in range(total)]
-        values = values + lax.ppermute(values, ("af", "sa"), pairs)
-        step *= 2
-    return values
+
+
+def exchange(values):
+    return send(values).astype(jnp.float32)
+
+
+def add_partner(values, step, total):
+    pairs = [(i, i ^ step) for i in range(total)]
+    return values + lax.ppermute(values, ("af", "sa"), pairs)
+
+
+def ring_pairs(c, ring):
+    way = 1 if c % 2 == 0 else -1
+    return [(i, (i + 2 * way) % ring) for i in range(ring)]
+
+
+def slot_ranks(c, ring):
+    chips = ring // 2
+    place = lax.axis_index("sa")
+    way = 1 if c % 2 == 0 else -1
+    steps = jnp.arange(chips, dtype=jnp.int32) * (2 * way)
+    same = (place - steps + 2 * ring) % ring
+    return jnp.concatenate([same, same ^ 1]).astype(jnp.int32)
 
 
 def on_device(data_r, data_i, wave_r, wave_i, primaries_r, primaries_i, *, sizes):
     parts, ring = sizes
+    total = parts * ring
     count, rows, n = data_r.shape
-    total_f = count * parts
     span = count // CHUNKS
-    wholes = []
+    chunks = []
     for c in range(CHUNKS):
         cut = slice(c * span, (c + 1) * span)
-        mine = jnp.stack([data_r[cut], data_i[cut]])
-        if rows % 16 == 0:
-            wholes.append(lax.all_gather(mine, "sa"))
-        else:
-            wholes.append(lax.all_gather(mine, "sa", axis=2, tiled=True))
-    current = (primaries_r, primaries_i)
-    sums = []
-    for _ in range(ITERS):
+        chunks.append(jnp.stack([data_r[cut], data_i[cut]]))
+    ring_form = 4 < ring <= MOST_RING and rows % 16 == 0
+    ranks = [slot_ranks(c, ring) if ring_form else None for c in range(CHUNKS)]
+    wholes = [None] * CHUNKS
+
+    def step(c, current):
+        return product(c, wave_r, wave_i, current, data_r, data_i, wholes[c], parts, ranks[c])
+
+    start = (primaries_r, primaries_i)
+    firsts = [None] * CHUNKS
+    if ring_form:
+        swap = [(i, i ^ 1) for i in range(ring)]
+        chips = ring // 2
+        before = None
+        for c in range(CHUNKS):
+            slots = [chunks[c]]
+            if c:
+                slots[0] = after(slots[0], before[-2])
+            for d in range(1, chips):
+                source = slots[-1]
+                if d == chips - 1 and c:
+                    source = after(source, firsts[c - 1][0])
+                slots.append(lax.ppermute(source, "sa", ring_pairs(c, ring)))
+                if d == 1 and c:
+                    firsts[c - 1] = step(c - 1, start)
+            before = slots
+            wholes[c] = slots + [lax.ppermute(slot, "sa", swap) for slot in slots]
+        firsts[-1] = step(CHUNKS - 1, start)
+    else:
+        for c in range(CHUNKS):
+            if rows % 16 == 0:
+                wholes[c] = lax.all_gather(chunks[c], "sa")
+            else:
+                wholes[c] = lax.all_gather(chunks[c], "sa", axis=2, tiled=True)
+            firsts[c] = step(c, start)
+    sums = [sum(jnp.sum(s) for _, s in firsts)]
+    pieces = [exchange(z) for z, _ in firsts]
+    shares = CHUNKS // GROUPS
+    for iteration in range(1, ITERS):
+        groups = transform(pieces, rows, GROUPS)
         pieces, partials = [], []
-        for c in range(CHUNKS):
-            z, s = product(c, wave_r, wave_i, current, data_r, data_i, wholes[c], parts)
-            pieces.append(exchange(z))
-            partials.append(s)
+        for g, group in enumerate(groups):
+            if g > 1:
+                group = after(group, latest)
+            current = exchange(group)
+            for c in range(g * shares, (g + 1) * shares):
+                latest, s = step(c, current)
+                pieces.append(exchange(latest))
+                partials.append(s)
         sums.append(sum(jnp.sum(s) for s in partials))
-        current = exchange(transform(pieces, rows))
-    misfit = everywhere(jnp.stack(sums), sizes) / (total_f * n * n)
-    scale = jnp.exp2(current[:, 2 * count] - TOP)[:, None]
+    values = jnp.stack(sums)
+    hop = 1
+    while hop < total:
+        values = add_partner(values, hop, total)
+        if hop == 2:
+            pieces[-1] = after(pieces[-1], values)
+        hop *= 2
+    misfit = values / (count * parts * n * n)
+    last = exchange(transform(pieces, rows, 1)[0])
+    scale = jnp.exp2(last[:, 2 * count] - TOP)[:, None]
 
     def whole_rows(part):
         return (part * scale).transpose(1, 2, 0, 3).reshape(count, rows, n)
 
-    return whole_rows(current[:, :count]), whole_rows(current[:, count : 2 * count]), misfit
+    return whole_rows(last[:, :count]), whole_rows(last[:, count : 2 * count]), misfit
 
 
 def solution(mesh):

time: 377 us -> 351 us (0.931)
  starting transfers between devices: 40 us -> 72.2 us
  blocking collectives: 28.3 us -> 0 us
  waiting for transfers between devices: 173 us -> 146 us
  between operations: 19.1 us -> 6.33 us
  other arithmetic: 45.9 us -> 50.4 us
    all_gather x4 -> x0, waiting for transfers between devices: 153 us -> none  [on_device(): wholes.append(lax.all_gather(mine, 'sa'))]
    ppermute x5 -> x33, waiting for transfers between devices: 10.9 us -> 124 us  [the longest x12 96.5 us: on_device(): slots.append(lax.ppermute(source, 'sa', ring_pairs(c, ring)))]
    all_to_all x1 -> x0, blocking collectives: 28.3 us -> none  [exchange(): lax.all_to_all(values.astype(jnp.float16), 'af', split_axis=0, concat_axi...]
    ppermute x5 -> x33, starting transfers between devices: 5.47 us -> 31 us  [the longest x12 23.8 us: on_device(): slots.append(lax.ppermute(source, 'sa', ring_pairs(c, ring)))]
    all_to_all x9 -> x11, waiting for transfers between devices: 9.12 us -> 21.6 us  [send(): lax.all_to_all(values.astype(jnp.float16), 'af', split_axis=0, concat_axi...]
    all_to_all x9 -> x11, starting transfers between devices: 34.4 us -> 41.2 us  [send(): lax.all_to_all(values.astype(jnp.float16), 'af', split_axis=0, concat_axi...]
    convert_element_type x20 -> x22, other arithmetic: 36 us -> 39.6 us  [the longest x11 27.3 us: send(): values.astype(jnp.float16)]
  transfers between devices with their start and end apart: 18 -> 44, of which waited for: 11 -> 21; matrix products, arithmetic and copies ran while one was open for 8% -> 11% of each run, Pallas kernels for 12% -> 15%
where the time goes in v2:
time: 351 us; the launch traced here: 349 us
  waiting for transfers between devices  146 us (42%)
  starting transfers between devices  72.2 us (21%)
  Pallas kernels  66 us (19%)
  other arithmetic  50.4 us (14%)
  local copies, waits for them, and re-layouts  8.01 us (2%)
  between operations  6.33 us (2%)
    ppermute x12, waiting for transfers between devices, on_device(): slots.append(lax.ppermute(source, 'sa', ring_pairs(c, ring)))  96.5 us
    pallas_call x8, Pallas kernels, product(): pl.pallas_call(kernel, grid=(span,), in_specs=[smem, smem] + cur + [own,...  51.6 us
    all_to_all x11, starting transfers between devices, send(): lax.all_to_all(values.astype(jnp.float16), 'af', split_axis=0, concat_axi...  41.2 us
    ppermute x5, waiting for transfers between devices, add_partner(): return values + lax.ppermute(values, ('af', 'sa'), pairs)  27.8 us
    convert_element_type x11, other arithmetic, send(): values.astype(jnp.float16)  27.3 us
    ppermute x12, starting transfers between devices, on_device(): slots.append(lax.ppermute(source, 'sa', ring_pairs(c, ring)))  23.8 us
    all_to_all x11, waiting for transfers between devices, send(): lax.all_to_all(values.astype(jnp.float16), 'af', split_axis=0, concat_axi...  21.6 us
    pallas_call x2, Pallas kernels, transform(): pl.pallas_call(partial(transform_kernel, parts=parts, count=count, span=s...  14.4 us
  transfers between devices with their start and end apart: 44, of which 21 were waited for; matrix products, arithmetic and copies ran while one was open for 11% of the time, Pallas kernels for 15%

profile of v2, /device:TPU:0, one launch (start us, length us, event | category | flops | bytes accessed | tf_op | source)
XLA Modules:
  0.0 348.9 jit_solution(5144391570142069322)
XLA Ops:
  0.6 2.5 slice_bitcast_fusion
  3.2 3.1 collective-permute-start
  6.3 13.9 %collective-permute-done.refs_8_.refs_9_ = bf16[2,4,64,512]{3,2,1,0:T(8,128)(2,1)S(1)} collective-permute-done((bf16[2,4,64,512]{3,2,1,0:T(8,128)(2,1)S(1)}, bf16[2,4,64,512]{3,2,1,0:T(8,128)(2,1)S(1)}, u32[]{:S(2)}, u32[]{:S(2)}) %collective-permute-start) | collective-permute-done | bytes 524320 | tf_op jit(solution)/shard_map/ppermute | solution.py:342
  20.3 15.0 %collective-permute-done.1.refs_9_.refs_10_ = bf16[2,4,64,512]{3,2,1,0:T(8,128)(2,1)S(1)} collective-permute-done((bf16[2,4,64,512]{3,2,1,0:T(8,128)(2,1)S(1)}, bf16[2,4,64,512]{3,2,1,0:T(8,128)(2,1)S(1)}, u32[]{:S(2)}, u32[]{:S(2)}) %collective-permute-start.1) | collective-permute-done | bytes 524320 | tf_op jit(solution)/shard_map/ppermute | solution.py:342
  35.3 3.9 %collective-permute-start.7 = (bf16[2,4,64,512]{3,2,1,0:T(8,128)(2,1)S(1)}, bf16[2,4,64,512]{3,2,1,0:T(8,128)(2,1)}, u32[]{:S(2)}, u32[]{:S(2)}) collective-permute-start(bf16[2,4,64,512]{3,2,1,0:T(8,128)(2,1)S(1)} %pad_maximum_fusion.1.refs_7_.refs_8_), channel_id=1, source_target_pairs={{0,6},{1,7},{2,0},{3,1},{4,2},{5,3},{6,4},{7,5},{8,14},{9,15},{10,... | collective-permute-start | bytes 1572872 | tf_op jit(solution)/shard_map/ppermute | solution.py:342
  39.7 12.1 %collective-permute-done.2.refs_10_.refs_11_ = bf16[2,4,64,512]{3,2,1,0:T(8,128)(2,1)S(1)} collective-permute-done((bf16[2,4,64,512]{3,2,1,0:T(8,128)(2,1)S(1)}, bf16[2,4,64,512]{3,2,1,0:T(8,128)(2,1)S(1)}, u32[]{:S(2)}, u32[]{:S(2)}) %collective-permute-start.2) | collective-permute-done | bytes 524320 | tf_op jit(solution)/shard_map/ppermute | solution.py:342
  51.8 7.0 %collective-permute-done.7.refs_8_.refs_9_ = bf16[2,4,64,512]{3,2,1,0:T(8,128)(2,1)} collective-permute-done((bf16[2,4,64,512]{3,2,1,0:T(8,128)(2,1)S(1)}, bf16[2,4,64,512]{3,2,1,0:T(8,128)(2,1)}, u32[]{:S(2)}, u32[]{:S(2)}) %collective-permute-start.7) | collective-permute-done | bytes 524320 | tf_op jit(solution)/shard_map/ppermute | solution.py:342
  62.2 6.4 %product_0_0.1 = (f32[4,4,17,8,128]{4,3,2,1,0:T(8,128)}, f32[4,8,128]{2,1,0:T(8,128)}) custom-call(f32[16]{0:T(128)} %refs_0_.15, f32[16]{0:T(128)} %refs_1_.15, f32[16,64,512]{2,1,0:T(8,128)} %refs_2_.7, f32[16,64,512]{2,1,0:T(8,128)} %refs_3_.7, bf16[16,64,512]{2,1,0:T(8,128)(2,1)} %refs_5_.15, bf16[16,64,512]{2,1,0:T(8,128)(2,1)} %refs_6_.7, ...), custom_call_target="tpu_custom_call" | custom-call | flops 1073741824 | bytes 6291456 | tf_op jit(solution)/shard_map/product_0_0/pallas_call | solution.py:182
  68.6 2.7 collective-permute-done.8.refs_9_.refs_10_
  71.3 3.2 collective-permute-start.9
  76.3 10.8 %collective-permute-done.9.refs_10_.refs_11_ = bf16[2,4,64,512]{3,2,1,0:T(8,128)(2,1)S(1)} collective-permute-done((bf16[2,4,64,512]{3,2,1,0:T(8,128)(2,1)}, bf16[2,4,64,512]{3,2,1,0:T(8,128)(2,1)S(1)}, u32[]{:S(2)}, u32[]{:S(2)}) %collective-permute-start.9) | collective-permute-done | bytes 524320 | tf_op jit(solution)/shard_map/ppermute | solution.py:342
  87.1 7.8 %collective-permute-done.14.refs_8_.refs_9_ = bf16[2,4,64,512]{3,2,1,0:T(8,128)(2,1)S(1)} collective-permute-done((bf16[2,4,64,512]{3,2,1,0:T(8,128)(2,1)S(1)}, bf16[2,4,64,512]{3,2,1,0:T(8,128)(2,1)S(1)}, u32[]{:S(2)}, u32[]{:S(2)}) %collective-permute-start.14) | collective-permute-done | bytes 524320 | tf_op jit(solution)/shard_map/ppermute | solution.py:342
  94.9 2.4 collective-permute-start.15
  98.8 6.4 %product_1_0.1 = (f32[4,4,17,8,128]{4,3,2,1,0:T(8,128)}, f32[4,8,128]{2,1,0:T(8,128)}) custom-call(f32[16]{0:T(128)} %refs_0_.15, f32[16]{0:T(128)} %refs_1_.15, f32[16,64,512]{2,1,0:T(8,128)} %refs_2_.7, f32[16,64,512]{2,1,0:T(8,128)} %refs_3_.7, bf16[16,64,512]{2,1,0:T(8,128)(2,1)} %refs_5_.15, bf16[16,64,512]{2,1,0:T(8,128)(2,1)} %refs_6_.7, ...), custom_call_target="tpu_custom_call" | custom-call | flops 1073741824 | bytes 6291456 | tf_op jit(solution)/shard_map/product_1_0/pallas_call | solution.py:182
  105.2 3.6 %collective-permute-done.15.refs_9_.refs_10_ = bf16[2,4,64,512]{3,2,1,0:T(8,128)(2,1)S(1)} collective-permute-done((bf16[2,4,64,512]{3,2,1,0:T(8,128)(2,1)S(1)}, bf16[2,4,64,512]{3,2,1,0:T(8,128)(2,1)S(1)}, u32[]{:S(2)}, u32[]{:S(2)}) %collective-permute-start.15) | collective-permute-done | bytes 524320 | tf_op jit(solution)/shard_map/ppermute | solution.py:342
  110.0 3.7 %collective-permute-start.21 = (bf16[2,4,64,512]{3,2,1,0:T(8,128)(2,1)S(1)}, bf16[2,4,64,512]{3,2,1,0:T(8,128)(2,1)}, u32[]{:S(2)}, u32[]{:S(2)}) collective-permute-start(bf16[2,4,64,512]{3,2,1,0:T(8,128)(2,1)S(1)} %pad_maximum_fusion.3.refs_7_.refs_8_), channel_id=1, source_target_pairs={{0,6},{1,7},{2,0},{3,1},{4,2},{5,3},{6,4},{7,5},{8,14},{9,15},{10,... | collective-permute-start | bytes 1572872 | tf_op jit(solution)/shard_map/ppermute | solution.py:342
  114.3 11.1 %collective-permute-done.16.refs_10_.refs_11_ = bf16[2,4,64,512]{3,2,1,0:T(8,128)(2,1)S(1)} collective-permute-done((bf16[2,4,64,512]{3,2,1,0:T(8,128)(2,1)S(1)}, bf16[2,4,64,512]{3,2,1,0:T(8,128)(2,1)S(1)}, u32[]{:S(2)}, u32[]{:S(2)}) %collective-permute-start.16) | collective-permute-done | bytes 524320 | tf_op jit(solution)/shard_map/ppermute | solution.py:342
  125.4 7.2 %collective-permute-done.21.refs_8_.refs_9_ = bf16[2,4,64,512]{3,2,1,0:T(8,128)(2,1)} collective-permute-done((bf16[2,4,64,512]{3,2,1,0:T(8,128)(2,1)S(1)}, bf16[2,4,64,512]{3,2,1,0:T(8,128)(2,1)}, u32[]{:S(2)}, u32[]{:S(2)}) %collective-permute-start.21) | collective-permute-done | bytes 524320 | tf_op jit(solution)/shard_map/ppermute | solution.py:342
  136.1 3.5 all-to-all-start
  139.7 6.4 %product_2_0.1 = (f32[4,4,17,8,128]{4,3,2,1,0:T(8,128)}, f32[4,8,128]{2,1,0:T(8,128)}) custom-call(f32[16]{0:T(128)} %refs_0_.15, f32[16]{0:T(128)} %refs_1_.15, f32[16,64,512]{2,1,0:T(8,128)} %refs_2_.7, f32[16,64,512]{2,1,0:T(8,128)} %refs_3_.7, bf16[16,64,512]{2,1,0:T(8,128)(2,1)} %refs_5_.15, bf16[16,64,512]{2,1,0:T(8,128)(2,1)} %refs_6_.7, ...), custom_call_target="tpu_custom_call" | custom-call | flops 1073741824 | bytes 6291456 | tf_op jit(solution)/shard_map/product_2_0/pallas_call | solution.py:182
  146.3 4.1 %collective-permute-start.23 = (bf16[2,4,64,512]{3,2,1,0:T(8,128)(2,1)}, bf16[2,4,64,512]{3,2,1,0:T(8,128)(2,1)S(1)}, u32[]{:S(2)}, u32[]{:S(2)}) collective-permute-start(bf16[2,4,64,512]{3,2,1,0:T(8,128)(2,1)} %collective-permute-done.22.refs_9_.refs_10_), channel_id=1, source_target_pairs={{0,6},{1,7},{2,0},{3,1},{4,2},{5,3},{6,4},{7,5},{8,14},{9,15},{10,... | collective-permute-start | bytes 1572872 | tf_op jit(solution)/shard_map/ppermute | solution.py:342
  152.6 3.5 all-to-all-start.1
  156.7 5.0 %collective-permute-done.23.refs_10_.refs_11_ = bf16[2,4,64,512]{3,2,1,0:T(8,128)(2,1)S(1)} collective-permute-done((bf16[2,4,64,512]{3,2,1,0:T(8,128)(2,1)}, bf16[2,4,64,512]{3,2,1,0:T(8,128)(2,1)S(1)}, u32[]{:S(2)}, u32[]{:S(2)}) %collective-permute-start.23) | collective-permute-done | bytes 524320 | tf_op jit(solution)/shard_map/ppermute | solution.py:342
  164.1 3.5 all-to-all-start.2
  168.4 6.4 %product_3_0.1 = (f32[4,4,17,8,128]{4,3,2,1,0:T(8,128)}, f32[4,8,128]{2,1,0:T(8,128)}) custom-call(f32[16]{0:T(128)} %refs_0_.15, f32[16]{0:T(128)} %refs_1_.15, f32[16,64,512]{2,1,0:T(8,128)} %refs_2_.7, f32[16,64,512]{2,1,0:T(8,128)} %refs_3_.7, bf16[16,64,512]{2,1,0:T(8,128)(2,1)} %refs_5_.15, bf16[16,64,512]{2,1,0:T(8,128)(2,1)} %refs_6_.7, ...), custom_call_target="tpu_custom_call" | custom-call | flops 1073741824 | bytes 6291456 | tf_op jit(solution)/shard_map/product_3_0/pallas_call | solution.py:182
  177.0 4.2 %all-to-all-start.3 = ((f16[4,4,17,8,128]{4,3,2,1,0:T(8,128)(2,1)}), f16[4,4,17,8,128]{4,3,2,1,0:T(8,128)(2,1)S(1)}, u32[]{:S(2)}, u32[]{:S(2)}) async-start(f16[4,4,17,8,128]{4,3,2,1,0:T(8,128)(2,1)} %convert_element_type.72), calls=%async_computation.3 | async-start | bytes 1114112 | tf_op jit(solution)/shard_map/all_to_all | solution.py:284
  184.4 5.2 %all-to-all-done.3 = f16[4,4,17,8,128]{4,3,2,1,0:T(8,128)(2,1)S(1)} async-done(((f16[4,4,17,8,128]{4,3,2,1,0:T(8,128)(2,1)}), f16[4,4,17,8,128]{4,3,2,1,0:T(8,128)(2,1)S(1)}, u32[]{:S(2)}, u32[]{:S(2)}) %all-to-all-start.3) | async-done | bytes 557088 | tf_op jit(solution)/shard_map/all_to_all | solution.py:284
  190.6 7.2 %transform.2 = (f32[4,17,64,128]{3,2,1,0:T(8,128)}, f32[4,17,64,128]{3,2,1,0:T(8,128)}) custom-call(f32[4,4,17,8,128]{4,3,2,1,0:T(8,128)} %convert_element_type.67.refs_0_.refs_1_.refs_2_, f32[4,4,17,8,128]{4,3,2,1,0:T(8,128)} %convert_element_type.67.refs_0_.refs_1_.refs_2_, f32[4,4,17,8,128]{4,3,2,1,0:T(8,128)} %convert_element_type.67.refs_0_.refs_1_.refs_2_, ...), custom_call_target="tpu_custom_call" | custom-call | tf_op jit(solution)/shard_map/transform/pallas_call | solution.py:265
  197.8 2.9 convert_element_type.74
  200.7 3.5 %all-to-all-start.4 = ((f16[4,17,64,128]{3,2,1,0:T(8,128)(2,1)}), f16[4,17,64,128]{3,2,1,0:T(8,128)(2,1)S(1)}, u32[]{:S(2)}, u32[]{:S(2)}) async-start(f16[4,17,64,128]{3,2,1,0:T(8,128)(2,1)} %convert_element_type.74), calls=%async_computation.4 | async-start | bytes 2228224 | tf_op jit(solution)/shard_map/all_to_all | solution.py:284
  204.3 2.9 convert_element_type.80
  207.2 10.7 %all-to-all-done.4 = f16[4,17,64,128]{3,2,1,0:T(8,128)(2,1)S(1)} async-done(((f16[4,17,64,128]{3,2,1,0:T(8,128)(2,1)}), f16[4,17,64,128]{3,2,1,0:T(8,128)(2,1)S(1)}, u32[]{:S(2)}, u32[]{:S(2)}) %all-to-all-start.4) | async-done | bytes 1114144 | tf_op jit(solution)/shard_map/all_to_all | solution.py:284
  217.8 3.5 %all-to-all-start.7 = ((f16[4,17,64,128]{3,2,1,0:T(8,128)(2,1)}), f16[4,17,64,128]{3,2,1,0:T(8,128)(2,1)S(1)}, u32[]{:S(2)}, u32[]{:S(2)}) async-start(f16[4,17,64,128]{3,2,1,0:T(8,128)(2,1)} %convert_element_type.80), calls=%async_computation.7 | async-start | bytes 2228224 | tf_op jit(solution)/shard_map/all_to_all | solution.py:284
  222.9 6.5 %product_1_1.1 = (f32[4,4,17,8,128]{4,3,2,1,0:T(8,128)}, f32[4,8,128]{2,1,0:T(8,128)}) custom-call(f32[16]{0:T(128)} %refs_0_.15, f32[16]{0:T(128)} %refs_1_.15, f32[4,17,64,128]{3,2,1,0:T(8,128)} %convert_element_type.75.refs_2_.refs_3_.refs_4_, f32[4,17,64,128]{3,2,1,0:T(8,128)} %convert_element_type.75.refs_2_.refs_3_.refs_4_, ...), custom_call_target="tpu_custom_call" | custom-call | flops 1073741824 | bytes 6291456 | tf_op jit(solution)/shard_map/product_1_1/pallas_call | solution.py:182
  231.6 3.6 %all-to-all-done.7 = f16[4,17,64,128]{3,2,1,0:T(8,128)(2,1)S(1)} async-done(((f16[4,17,64,128]{3,2,1,0:T(8,128)(2,1)}), f16[4,17,64,128]{3,2,1,0:T(8,128)(2,1)S(1)}, u32[]{:S(2)}, u32[]{:S(2)}) %all-to-all-start.7) | async-done | bytes 1114144 | tf_op jit(solution)/shard_map/all_to_all | solution.py:284
  235.2 3.5 all-to-all-start.6
  238.6 6.5 %product_0_1.1 = (f32[4,4,17,8,128]{4,3,2,1,0:T(8,128)}, f32[4,8,128]{2,1,0:T(8,128)}) custom-call(f32[16]{0:T(128)} %refs_0_.15, f32[16]{0:T(128)} %refs_1_.15, f32[4,17,64,128]{3,2,1,0:T(8,128)} %convert_element_type.75.refs_2_.refs_3_.refs_4_, f32[4,17,64,128]{3,2,1,0:T(8,128)} %convert_element_type.75.refs_2_.refs_3_.refs_4_, ...), custom_call_target="tpu_custom_call" | custom-call | flops 1073741824 | bytes 6291456 | tf_op jit(solution)/shard_map/product_0_1/pallas_call | solution.py:182
  247.3 4.1 %all-to-all-start.5 = ((f16[4,4,17,8,128]{4,3,2,1,0:T(8,128)(2,1)}), f16[4,4,17,8,128]{4,3,2,1,0:T(8,128)(2,1)S(1)}, u32[]{:S(2)}, u32[]{:S(2)}) async-start(f16[4,4,17,8,128]{4,3,2,1,0:T(8,128)(2,1)} %convert_element_type.76), calls=%async_computation.5 | async-start | bytes 1114112 | tf_op jit(solution)/shard_map/all_to_all | solution.py:284
  253.0 6.5 %product_3_1.1 = (f32[4,4,17,8,128]{4,3,2,1,0:T(8,128)}, f32[4,8,128]{2,1,0:T(8,128)}) custom-call(f32[16]{0:T(128)} %refs_0_.15, f32[16]{0:T(128)} %refs_1_.15, f32[4,17,64,128]{3,2,1,0:T(8,128)} %convert_element_type.81.refs_2_.refs_3_.refs_4_, f32[4,17,64,128]{3,2,1,0:T(8,128)} %convert_element_type.81.refs_2_.refs_3_.refs_4_, ...), custom_call_target="tpu_custom_call" | custom-call | flops 1073741824 | bytes 6291456 | tf_op jit(solution)/shard_map/product_3_1/pallas_call | solution.py:182
  261.8 4.2 %all-to-all-start.9 = ((f16[4,4,17,8,128]{4,3,2,1,0:T(8,128)(2,1)}), f16[4,4,17,8,128]{4,3,2,1,0:T(8,128)(2,1)S(1)}, u32[]{:S(2)}, u32[]{:S(2)}) async-start(f16[4,4,17,8,128]{4,3,2,1,0:T(8,128)(2,1)} %convert_element_type.84), calls=%async_computation.9 | async-start | bytes 1114112 | tf_op jit(solution)/shard_map/all_to_all | solution.py:284
  272.3 6.5 %product_2_1.1 = (f32[4,4,17,8,128]{4,3,2,1,0:T(8,128)}, f32[4,8,128]{2,1,0:T(8,128)}) custom-call(f32[16]{0:T(128)} %refs_0_.15, f32[16]{0:T(128)} %refs_1_.15, f32[4,17,64,128]{3,2,1,0:T(8,128)} %convert_element_type.81.refs_2_.refs_3_.refs_4_, f32[4,17,64,128]{3,2,1,0:T(8,128)} %convert_element_type.81.refs_2_.refs_3_.refs_4_, ...), custom_call_target="tpu_custom_call" | custom-call | flops 1073741824 | bytes 6291456 | tf_op jit(solution)/shard_map/product_2_1/pallas_call | solution.py:182
  285.5 4.2 %all-to-all-start.8 = ((f16[4,4,17,8,128]{4,3,2,1,0:T(8,128)(2,1)}), f16[4,4,17,8,128]{4,3,2,1,0:T(8,128)(2,1)S(1)}, u32[]{:S(2)}, u32[]{:S(2)}) async-start(f16[4,4,17,8,128]{4,3,2,1,0:T(8,128)(2,1)} %convert_element_type.82), calls=%async_computation.8 | async-start | bytes 1114112 | tf_op jit(solution)/shard_map/all_to_all | solution.py:284
  289.8 3.6 %collective-permute-done.29 = f32[2]{0:T(128)S(1)} collective-permute-done((f32[2]{0:T(128)S(1)}, f32[2]{0:T(128)S(1)}, u32[]{:S(2)}, u32[]{:S(2)}) %collective-permute-start.29) | collective-permute-done | bytes 40 | tf_op jit(solution)/shard_map/ppermute | solution.py:295
  299.8 7.2 %transform.3 = f32[4,33,64,128]{3,2,1,0:T(8,128)} custom-call(f32[4,4,17,8,128]{4,3,2,1,0:T(8,128)} %convert_element_type.77.refs_0_.refs_1_.refs_2_, f32[4,4,17,8,128]{4,3,2,1,0:T(8,128)} %convert_element_type.77.refs_0_.refs_1_.refs_2_, f32[4,4,17,8,128]{4,3,2,1,0:T(8,128)} %convert_element_type.77.refs_0_.refs_1_.refs_2_, ...), custom_call_target="tpu_custom_call" | custom-call | tf_op jit(solution)/shard_map/transform/pallas_call | solution.py:265
  307.0 4.2 %convert_element_type.86 = f16[4,33,64,128]{3,2,1,0:T(8,128)(2,1)} convert(f32[4,33,64,128]{3,2,1,0:T(8,128)} %transform.3) | non-fusion elementwise | flops 1081344 | bytes 6488064 | tf_op jit(solution)/shard_map/convert_element_type | solution.py:285
  311.2 3.6 %all-to-all-start.10 = ((f16[4,33,64,128]{3,2,1,0:T(8,128)(2,1)}), f16[4,33,64,128]{3,2,1,0:T(8,128)(2,1)S(1)}, u32[]{:S(2)}, u32[]{:S(2)}) async-start(f16[4,33,64,128]{3,2,1,0:T(8,128)(2,1)} %convert_element_type.86), calls=%async_computation.10 | async-start | bytes 4325376 | tf_op jit(solution)/shard_map/all_to_all | solution.py:284
  316.2 3.1 collective-permute-done.30
  321.3 19.0 %collective-permute-done.31 = f32[2]{0:T(128)S(1)} collective-permute-done((f32[2]{0:T(128)S(1)}, f32[2]{0:T(128)S(1)}, u32[]{:S(2)}, u32[]{:S(2)}) %collective-permute-start.31) | collective-permute-done | bytes 40 | tf_op jit(solution)/shard_map/ppermute | solution.py:295
  (143 shorter events, 61.0 us)
Async XLA Ops:
  3.2 58.2 %copy-start = (bf16[2,4,64,512]{3,2,1,0:T(8,128)(2,1)}, bf16[2,4,64,512]{3,2,1,0:T(8,128)(2,1)S(1)}, u32[]{:S(2)}) copy-start(bf16[2,4,64,512]{3,2,1,0:T(8,128)(2,1)S(1)} %pad_maximum_fusion.refs_7_.refs_8_) | copy-start | bytes 1572868
  3.2 17.1 %collective-permute-start = (bf16[2,4,64,512]{3,2,1,0:T(8,128)(2,1)S(1)}, bf16[2,4,64,512]{3,2,1,0:T(8,128)(2,1)S(1)}, u32[]{:S(2)}, u32[]{:S(2)}) collective-permute-start(bf16[2,4,64,512]{3,2,1,0:T(8,128)(2,1)S(1)} %pad_maximum_fusion.refs_7_.refs_8_), channel_id=1, source_target_pairs={{0,2},{1,3},{2,4},{3,5},{4,6},{5,7},{6,0},{7,1},{8,10},{9,11},{10,... | collective-permute-start | bytes 1572872 | tf_op jit(solution)/shard_map/ppermute | solution.py:342
  20.2 41.2 %copy-start.4 = (bf16[2,4,64,512]{3,2,1,0:T(8,128)(2,1)}, bf16[2,4,64,512]{3,2,1,0:T(8,128)(2,1)S(1)}, u32[]{:S(2)}) copy-start(bf16[2,4,64,512]{3,2,1,0:T(8,128)(2,1)S(1)} %collective-permute-done.refs_8_.refs_9_) | copy-start | bytes 1572868
  20.3 15.0 %collective-permute-start.1 = (bf16[2,4,64,512]{3,2,1,0:T(8,128)(2,1)S(1)}, bf16[2,4,64,512]{3,2,1,0:T(8,128)(2,1)S(1)}, u32[]{:S(2)}, u32[]{:S(2)}) collective-permute-start(bf16[2,4,64,512]{3,2,1,0:T(8,128)(2,1)S(1)} %collective-permute-done.refs_8_.refs_9_), channel_id=1, source_target_pairs={{0,2},{1,3},{2,4},{3,5},{4,6},{5,7},{6,0},{7,1},{8,10},{9,11},{10,... | collective-permute-start | bytes 1572872 | tf_op jit(solution)/shard_map/ppermute | solution.py:342
  35.2 16.6 %collective-permute-start.2 = (bf16[2,4,64,512]{3,2,1,0:T(8,128)(2,1)S(1)}, bf16[2,4,64,512]{3,2,1,0:T(8,128)(2,1)S(1)}, u32[]{:S(2)}, u32[]{:S(2)}) collective-permute-start(bf16[2,4,64,512]{3,2,1,0:T(8,128)(2,1)S(1)} %collective-permute-done.1.refs_9_.refs_10_), channel_id=1, source_target_pairs={{0,2},{1,3},{2,4},{3,5},{4,6},{5,7},{6,0},{7,1},{8,10},{9,11},{10,... | collective-permute-start | bytes 1572872 | tf_op jit(solution)/shard_map/ppermute | solution.py:342
  35.3 40.4 %copy-start.2 = (bf16[2,4,64,512]{3,2,1,0:T(8,128)(2,1)}, bf16[2,4,64,512]{3,2,1,0:T(8,128)(2,1)S(1)}, u32[]{:S(2)}) copy-start(bf16[2,4,64,512]{3,2,1,0:T(8,128)(2,1)S(1)} %pad_maximum_fusion.1.refs_7_.refs_8_) | copy-start | bytes 1572868
  35.3 23.6 %collective-permute-start.7 = (bf16[2,4,64,512]{3,2,1,0:T(8,128)(2,1)S(1)}, bf16[2,4,64,512]{3,2,1,0:T(8,128)(2,1)}, u32[]{:S(2)}, u32[]{:S(2)}) collective-permute-start(bf16[2,4,64,512]{3,2,1,0:T(8,128)(2,1)S(1)} %pad_maximum_fusion.1.refs_7_.refs_8_), channel_id=1, source_target_pairs={{0,6},{1,7},{2,0},{3,1},{4,2},{5,3},{6,4},{7,5},{8,14},{9,15},{10,... | collective-permute-start | bytes 1572872 | tf_op jit(solution)/shard_map/ppermute | solution.py:342
  39.2 22.2 %collective-permute-start.3 = (bf16[2,4,64,512]{3,2,1,0:T(8,128)(2,1)S(1)}, bf16[2,4,64,512]{3,2,1,0:T(8,128)(2,1)S(1)}, u32[]{:S(2)}, u32[]{:S(2)}) collective-permute-start(bf16[2,4,64,512]{3,2,1,0:T(8,128)(2,1)S(1)} %pad_maximum_fusion.refs_7_.refs_8_), channel_id=1, source_target_pairs={{0,1},{1,0},{2,3},{3,2},{4,5},{5,4},{6,7},{7,6},{8,9},{9,8},{10,11... | collective-permute-start | bytes 1572872 | tf_op jit(solution)/shard_map/ppermute | solution.py:346
  39.2 22.2 %collective-permute-start.4 = (bf16[2,4,64,512]{3,2,1,0:T(8,128)(2,1)S(1)}, bf16[2,4,64,512]{3,2,1,0:T(8,128)(2,1)}, u32[]{:S(2)}, u32[]{:S(2)}) collective-permute-start(bf16[2,4,64,512]{3,2,1,0:T(8,128)(2,1)S(1)} %collective-permute-done.refs_8_.refs_9_), channel_id=1, source_target_pairs={{0,1},{1,0},{2,3},{3,2},{4,5},{5,4},{6,7},{7,6},{8,9},{9,8},{10,11... | collective-permute-start | bytes 1572872 | tf_op jit(solution)/shard_map/ppermute | solution.py:346
  39.7 21.7 %collective-permute-start.5 = (bf16[2,4,64,512]{3,2,1,0:T(8,128)(2,1)S(1)}, bf16[2,4,64,512]{3,2,1,0:T(8,128)(2,1)}, u32[]{:S(2)}, u32[]{:S(2)}) collective-permute-start(bf16[2,4,64,512]{3,2,1,0:T(8,128)(2,1)S(1)} %collective-permute-done.1.refs_9_.refs_10_), channel_id=1, source_target_pairs={{0,1},{1,0},{2,3},{3,2},{4,5},{5,4},{6,7},{7,6},{8,9},{9,8},{10,11... | collective-permute-start | bytes 1572872 | tf_op jit(solution)/shard_map/ppermute | solution.py:346
  51.8 9.6 %collective-permute-start.6 = (bf16[2,4,64,512]{3,2,1,0:T(8,128)(2,1)S(1)}, bf16[2,4,64,512]{3,2,1,0:T(8,128)(2,1)}, u32[]{:S(2)}, u32[]{:S(2)}) collective-permute-start(bf16[2,4,64,512]{3,2,1,0:T(8,128)(2,1)S(1)} %collective-permute-done.2.refs_10_.refs_11_), channel_id=1, source_target_pairs={{0,1},{1,0},{2,3},{3,2},{4,5},{5,4},{6,7},{7,6},{8,9},{9,8},{10,11... | collective-permute-start | bytes 1572872 | tf_op jit(solution)/shard_map/ppermute | solution.py:346
  58.8 12.5 %collective-permute-start.8 = (bf16[2,4,64,512]{3,2,1,0:T(8,128)(2,1)}, bf16[2,4,64,512]{3,2,1,0:T(8,128)(2,1)}, u32[]{:S(2)}, u32[]{:S(2)}) collective-permute-start(bf16[2,4,64,512]{3,2,1,0:T(8,128)(2,1)} %collective-permute-done.7.refs_8_.refs_9_), channel_id=1, source_target_pairs={{0,6},{1,7},{2,0},{3,1},{4,2},{5,3},{6,4},{7,5},{8,14},{9,15},{10,... | collective-permute-start | bytes 1572872 | tf_op jit(solution)/shard_map/ppermute | solution.py:342
  71.3 15.8 %collective-permute-start.9 = (bf16[2,4,64,512]{3,2,1,0:T(8,128)(2,1)}, bf16[2,4,64,512]{3,2,1,0:T(8,128)(2,1)S(1)}, u32[]{:S(2)}, u32[]{:S(2)}) collective-permute-start(bf16[2,4,64,512]{3,2,1,0:T(8,128)(2,1)} %collective-permute-done.8.refs_9_.refs_10_), channel_id=1, source_target_pairs={{0,6},{1,7},{2,0},{3,1},{4,2},{5,3},{6,4},{7,5},{8,14},{9,15},{10,... | collective-permute-start | bytes 1572872 | tf_op jit(solution)/shard_map/ppermute | solution.py:342
  75.6 19.3 %collective-permute-start.14 = (bf16[2,4,64,512]{3,2,1,0:T(8,128)(2,1)S(1)}, bf16[2,4,64,512]{3,2,1,0:T(8,128)(2,1)S(1)}, u32[]{:S(2)}, u32[]{:S(2)}) collective-permute-start(bf16[2,4,64,512]{3,2,1,0:T(8,128)(2,1)S(1)} %pad_maximum_fusion.2.refs_7_.refs_8_), channel_id=1, source_target_pairs={{0,2},{1,3},{2,4},{3,5},{4,6},{5,7},{6,0},{7,1},{8,10},{9,11},{10,... | collective-permute-start | bytes 1572872 | tf_op jit(solution)/shard_map/ppermute | solution.py:342
  75.7 22.3 %collective-permute-start.10 = (bf16[2,4,64,512]{3,2,1,0:T(8,128)(2,1)S(1)}, bf16[2,4,64,512]{3,2,1,0:T(8,128)(2,1)S(1)}, u32[]{:S(2)}, u32[]{:S(2)}) collective-permute-start(bf16[2,4,64,512]{3,2,1,0:T(8,128)(2,1)S(1)} %pad_maximum_fusion.1.refs_7_.refs_8_), channel_id=1, source_target_pairs={{0,1},{1,0},{2,3},{3,2},{4,5},{5,4},{6,7},{7,6},{8,9},{9,8},{10,11... | collective-permute-start | bytes 1572872 | tf_op jit(solution)/shard_map/ppermute | solution.py:346
  75.7 22.3 %collective-permute-start.11 = (bf16[2,4,64,512]{3,2,1,0:T(8,128)(2,1)}, bf16[2,4,64,512]{3,2,1,0:T(8,128)(2,1)}, u32[]{:S(2)}, u32[]{:S(2)}) collective-permute-start(bf16[2,4,64,512]{3,2,1,0:T(8,128)(2,1)} %collective-permute-done.7.refs_8_.refs_9_), channel_id=1, source_target_pairs={{0,1},{1,0},{2,3},{3,2},{4,5},{5,4},{6,7},{7,6},{8,9},{9,8},{10,11... | collective-permute-start | bytes 1572872 | tf_op jit(solution)/shard_map/ppermute | solution.py:346
  76.2 21.8 %collective-permute-start.12 = (bf16[2,4,64,512]{3,2,1,0:T(8,128)(2,1)}, bf16[2,4,64,512]{3,2,1,0:T(8,128)(2,1)}, u32[]{:S(2)}, u32[]{:S(2)}) collective-permute-start(bf16[2,4,64,512]{3,2,1,0:T(8,128)(2,1)} %collective-permute-done.8.refs_9_.refs_10_), channel_id=1, source_target_pairs={{0,1},{1,0},{2,3},{3,2},{4,5},{5,4},{6,7},{7,6},{8,9},{9,8},{10,11... | collective-permute-start | bytes 1572872 | tf_op jit(solution)/shard_map/ppermute | solution.py:346
  87.1 10.9 %collective-permute-start.13 = (bf16[2,4,64,512]{3,2,1,0:T(8,128)(2,1)S(1)}, bf16[2,4,64,512]{3,2,1,0:T(8,128)(2,1)}, u32[]{:S(2)}, u32[]{:S(2)}) collective-permute-start(bf16[2,4,64,512]{3,2,1,0:T(8,128)(2,1)S(1)} %collective-permute-done.9.refs_10_.refs_11_), channel_id=1, source_target_pairs={{0,1},{1,0},{2,3},{3,2},{4,5},{5,4},{6,7},{7,6},{8,9},{9,8},{10,11... | collective-permute-start | bytes 1572872 | tf_op jit(solution)/shard_map/ppermute | solution.py:346
  94.9 13.9 %collective-permute-start.15 = (bf16[2,4,64,512]{3,2,1,0:T(8,128)(2,1)S(1)}, bf16[2,4,64,512]{3,2,1,0:T(8,128)(2,1)S(1)}, u32[]{:S(2)}, u32[]{:S(2)}) collective-permute-start(bf16[2,4,64,512]{3,2,1,0:T(8,128)(2,1)S(1)} %collective-permute-done.14.refs_8_.refs_9_), channel_id=1, source_target_pairs={{0,2},{1,3},{2,4},{3,5},{4,6},{5,7},{6,0},{7,1},{8,10},{9,11},{10,... | collective-permute-start | bytes 1572872 | tf_op jit(solution)/shard_map/ppermute | solution.py:342
  108.8 16.6 %collective-permute-start.16 = (bf16[2,4,64,512]{3,2,1,0:T(8,128)(2,1)S(1)}, bf16[2,4,64,512]{3,2,1,0:T(8,128)(2,1)S(1)}, u32[]{:S(2)}, u32[]{:S(2)}) collective-permute-start(bf16[2,4,64,512]{3,2,1,0:T(8,128)(2,1)S(1)} %collective-permute-done.15.refs_9_.refs_10_), channel_id=1, source_target_pairs={{0,2},{1,3},{2,4},{3,5},{4,6},{5,7},{6,0},{7,1},{8,10},{9,11},{10,... | collective-permute-start | bytes 1572872 | tf_op jit(solution)/shard_map/ppermute | solution.py:342
  110.0 46.0 %copy-start.3 = (bf16[2,4,64,512]{3,2,1,0:T(8,128)(2,1)}, bf16[2,4,64,512]{3,2,1,0:T(8,128)(2,1)S(1)}, u32[]{:S(2)}) copy-start(bf16[2,4,64,512]{3,2,1,0:T(8,128)(2,1)S(1)} %pad_maximum_fusion.3.refs_7_.refs_8_) | copy-start | bytes 1572868
  110.0 22.7 %collective-permute-start.21 = (bf16[2,4,64,512]{3,2,1,0:T(8,128)(2,1)S(1)}, bf16[2,4,64,512]{3,2,1,0:T(8,128)(2,1)}, u32[]{:S(2)}, u32[]{:S(2)}) collective-permute-start(bf16[2,4,64,512]{3,2,1,0:T(8,128)(2,1)S(1)} %pad_maximum_fusion.3.refs_7_.refs_8_), channel_id=1, source_target_pairs={{0,6},{1,7},{2,0},{3,1},{4,2},{5,3},{6,4},{7,5},{8,14},{9,15},{10,... | collective-permute-start | bytes 1572872 | tf_op jit(solution)/shard_map/ppermute | solution.py:342
  113.7 25.9 %collective-permute-start.17 = (bf16[2,4,64,512]{3,2,1,0:T(8,128)(2,1)S(1)}, bf16[2,4,64,512]{3,2,1,0:T(8,128)(2,1)}, u32[]{:S(2)}, u32[]{:S(2)}) collective-permute-start(bf16[2,4,64,512]{3,2,1,0:T(8,128)(2,1)S(1)} %pad_maximum_fusion.2.refs_7_.refs_8_), channel_id=1, source_target_pairs={{0,1},{1,0},{2,3},{3,2},{4,5},{5,4},{6,7},{7,6},{8,9},{9,8},{10,11... | collective-permute-start | bytes 1572872 | tf_op jit(solution)/shard_map/ppermute | solution.py:346
  113.7 25.9 %collective-permute-start.18 = (bf16[2,4,64,512]{3,2,1,0:T(8,128)(2,1)S(1)}, bf16[2,4,64,512]{3,2,1,0:T(8,128)(2,1)}, u32[]{:S(2)}, u32[]{:S(2)}) collective-permute-start(bf16[2,4,64,512]{3,2,1,0:T(8,128)(2,1)S(1)} %collective-permute-done.14.refs_8_.refs_9_), channel_id=1, source_target_pairs={{0,1},{1,0},{2,3},{3,2},{4,5},{5,4},{6,7},{7,6},{8,9},{9,8},{10,11... | collective-permute-start | bytes 1572872 | tf_op jit(solution)/shard_map/ppermute | solution.py:346
  114.3 25.4 %collective-permute-start.19 = (bf16[2,4,64,512]{3,2,1,0:T(8,128)(2,1)S(1)}, bf16[2,4,64,512]{3,2,1,0:T(8,128)(2,1)}, u32[]{:S(2)}, u32[]{:S(2)}) collective-permute-start(bf16[2,4,64,512]{3,2,1,0:T(8,128)(2,1)S(1)} %collective-permute-done.15.refs_9_.refs_10_), channel_id=1, source_target_pairs={{0,1},{1,0},{2,3},{3,2},{4,5},{5,4},{6,7},{7,6},{8,9},{9,8},{10,11... | collective-permute-start | bytes 1572872 | tf_op jit(solution)/shard_map/ppermute | solution.py:346
  125.4 14.2 %collective-permute-start.20 = (bf16[2,4,64,512]{3,2,1,0:T(8,128)(2,1)S(1)}, bf16[2,4,64,512]{3,2,1,0:T(8,128)(2,1)}, u32[]{:S(2)}, u32[]{:S(2)}) collective-permute-start(bf16[2,4,64,512]{3,2,1,0:T(8,128)(2,1)S(1)} %collective-permute-done.16.refs_10_.refs_11_), channel_id=1, source_target_pairs={{0,1},{1,0},{2,3},{3,2},{4,5},{5,4},{6,7},{7,6},{8,9},{9,8},{10,11... | collective-permute-start | bytes 1572872 | tf_op jit(solution)/shard_map/ppermute | solution.py:346
  132.7 13.6 %collective-permute-start.22 = (bf16[2,4,64,512]{3,2,1,0:T(8,128)(2,1)}, bf16[2,4,64,512]{3,2,1,0:T(8,128)(2,1)}, u32[]{:S(2)}, u32[]{:S(2)}) collective-permute-start(bf16[2,4,64,512]{3,2,1,0:T(8,128)(2,1)} %collective-permute-done.21.refs_8_.refs_9_), channel_id=1, source_target_pairs={{0,6},{1,7},{2,0},{3,1},{4,2},{5,3},{6,4},{7,5},{8,14},{9,15},{10,... | collective-permute-start | bytes 1572872 | tf_op jit(solution)/shard_map/ppermute | solution.py:342
  136.1 16.4 %all-to-all-start = ((f16[4,4,17,8,128]{4,3,2,1,0:T(8,128)(2,1)}), f16[4,4,17,8,128]{4,3,2,1,0:T(8,128)(2,1)S(1)}, u32[]{:S(2)}, u32[]{:S(2)}) async-start(f16[4,4,17,8,128]{4,3,2,1,0:T(8,128)(2,1)} %convert_element_type.66), calls=%async_computation | async-start | bytes 1114112 | tf_op jit(solution)/shard_map/all_to_all | solution.py:284
  146.3 15.4 %collective-permute-start.23 = (bf16[2,4,64,512]{3,2,1,0:T(8,128)(2,1)}, bf16[2,4,64,512]{3,2,1,0:T(8,128)(2,1)S(1)}, u32[]{:S(2)}, u32[]{:S(2)}) collective-permute-start(bf16[2,4,64,512]{3,2,1,0:T(8,128)(2,1)} %collective-permute-done.22.refs_9_.refs_10_), channel_id=1, source_target_pairs={{0,6},{1,7},{2,0},{3,1},{4,2},{5,3},{6,4},{7,5},{8,14},{9,15},{10,... | collective-permute-start | bytes 1572872 | tf_op jit(solution)/shard_map/ppermute | solution.py:342
  152.6 11.6 %all-to-all-start.1 = ((f16[4,4,17,8,128]{4,3,2,1,0:T(8,128)(2,1)}), f16[4,4,17,8,128]{4,3,2,1,0:T(8,128)(2,1)S(1)}, u32[]{:S(2)}, u32[]{:S(2)}) async-start(f16[4,4,17,8,128]{4,3,2,1,0:T(8,128)(2,1)} %convert_element_type.68), calls=%async_computation.1 | async-start | bytes 1114112 | tf_op jit(solution)/shard_map/all_to_all | solution.py:284
  156.0 11.6 %collective-permute-start.24 = (bf16[2,4,64,512]{3,2,1,0:T(8,128)(2,1)S(1)}, bf16[2,4,64,512]{3,2,1,0:T(8,128)(2,1)S(1)}, u32[]{:S(2)}, u32[]{:S(2)}) collective-permute-start(bf16[2,4,64,512]{3,2,1,0:T(8,128)(2,1)S(1)} %pad_maximum_fusion.3.refs_7_.refs_8_), channel_id=1, source_target_pairs={{0,1},{1,0},{2,3},{3,2},{4,5},{5,4},{6,7},{7,6},{8,9},{9,8},{10,11... | collective-permute-start | bytes 1572872 | tf_op jit(solution)/shard_map/ppermute | solution.py:346
  156.1 11.5 %collective-permute-start.25 = (bf16[2,4,64,512]{3,2,1,0:T(8,128)(2,1)}, bf16[2,4,64,512]{3,2,1,0:T(8,128)(2,1)}, u32[]{:S(2)}, u32[]{:S(2)}) collective-permute-start(bf16[2,4,64,512]{3,2,1,0:T(8,128)(2,1)} %collective-permute-done.21.refs_8_.refs_9_), channel_id=1, source_target_pairs={{0,1},{1,0},{2,3},{3,2},{4,5},{5,4},{6,7},{7,6},{8,9},{9,8},{10,11... | collective-permute-start | bytes 1572872 | tf_op jit(solution)/shard_map/ppermute | solution.py:346
  156.6 11.0 %collective-permute-start.26 = (bf16[2,4,64,512]{3,2,1,0:T(8,128)(2,1)}, bf16[2,4,64,512]{3,2,1,0:T(8,128)(2,1)}, u32[]{:S(2)}, u32[]{:S(2)}) collective-permute-start(bf16[2,4,64,512]{3,2,1,0:T(8,128)(2,1)} %collective-permute-done.22.refs_9_.refs_10_), channel_id=1, source_target_pairs={{0,1},{1,0},{2,3},{3,2},{4,5},{5,4},{6,7},{7,6},{8,9},{9,8},{10,11... | collective-permute-start | bytes 1572872 | tf_op jit(solution)/shard_map/ppermute | solution.py:346
  161.7 6.0 %collective-permute-start.27 = (bf16[2,4,64,512]{3,2,1,0:T(8,128)(2,1)S(1)}, bf16[2,4,64,512]{3,2,1,0:T(8,128)(2,1)}, u32[]{:S(2)}, u32[]{:S(2)}) collective-permute-start(bf16[2,4,64,512]{3,2,1,0:T(8,128)(2,1)S(1)} %collective-permute-done.23.refs_10_.refs_11_), channel_id=1, source_target_pairs={{0,1},{1,0},{2,3},{3,2},{4,5},{5,4},{6,7},{7,6},{8,9},{9,8},{10,11... | collective-permute-start | bytes 1572872 | tf_op jit(solution)/shard_map/ppermute | solution.py:346
  164.1 12.8 %all-to-all-start.2 = ((f16[4,4,17,8,128]{4,3,2,1,0:T(8,128)(2,1)}), f16[4,4,17,8,128]{4,3,2,1,0:T(8,128)(2,1)S(1)}, u32[]{:S(2)}, u32[]{:S(2)}) async-start(f16[4,4,17,8,128]{4,3,2,1,0:T(8,128)(2,1)} %convert_element_type.70), calls=%async_computation.2 | async-start | bytes 1114112 | tf_op jit(solution)/shard_map/all_to_all | solution.py:284
  177.0 12.6 %all-to-all-start.3 = ((f16[4,4,17,8,128]{4,3,2,1,0:T(8,128)(2,1)}), f16[4,4,17,8,128]{4,3,2,1,0:T(8,128)(2,1)S(1)}, u32[]{:S(2)}, u32[]{:S(2)}) async-start(f16[4,4,17,8,128]{4,3,2,1,0:T(8,128)(2,1)} %convert_element_type.72), calls=%async_computation.3 | async-start | bytes 1114112 | tf_op jit(solution)/shard_map/all_to_all | solution.py:284
  200.7 17.1 %all-to-all-start.4 = ((f16[4,17,64,128]{3,2,1,0:T(8,128)(2,1)}), f16[4,17,64,128]{3,2,1,0:T(8,128)(2,1)S(1)}, u32[]{:S(2)}, u32[]{:S(2)}) async-start(f16[4,17,64,128]{3,2,1,0:T(8,128)(2,1)} %convert_element_type.74), calls=%async_computation.4 | async-start | bytes 2228224 | tf_op jit(solution)/shard_map/all_to_all | solution.py:284
  217.8 17.3 %all-to-all-start.7 = ((f16[4,17,64,128]{3,2,1,0:T(8,128)(2,1)}), f16[4,17,64,128]{3,2,1,0:T(8,128)(2,1)S(1)}, u32[]{:S(2)}, u32[]{:S(2)}) async-start(f16[4,17,64,128]{3,2,1,0:T(8,128)(2,1)} %convert_element_type.80), calls=%async_computation.7 | async-start | bytes 2228224 | tf_op jit(solution)/shard_map/all_to_all | solution.py:284
  235.2 12.1 %all-to-all-start.6 = ((f16[4,4,17,8,128]{4,3,2,1,0:T(8,128)(2,1)}), f16[4,4,17,8,128]{4,3,2,1,0:T(8,128)(2,1)S(1)}, u32[]{:S(2)}, u32[]{:S(2)}) async-start(f16[4,4,17,8,128]{4,3,2,1,0:T(8,128)(2,1)} %convert_element_type.78), calls=%async_computation.6 | async-start | bytes 1114112 | tf_op jit(solution)/shard_map/all_to_all | solution.py:284
  247.3 14.5 %all-to-all-start.5 = ((f16[4,4,17,8,128]{4,3,2,1,0:T(8,128)(2,1)}), f16[4,4,17,8,128]{4,3,2,1,0:T(8,128)(2,1)S(1)}, u32[]{:S(2)}, u32[]{:S(2)}) async-start(f16[4,4,17,8,128]{4,3,2,1,0:T(8,128)(2,1)} %convert_element_type.76), calls=%async_computation.5 | async-start | bytes 1114112 | tf_op jit(solution)/shard_map/all_to_all | solution.py:284
  261.8 23.7 %all-to-all-start.9 = ((f16[4,4,17,8,128]{4,3,2,1,0:T(8,128)(2,1)}), f16[4,4,17,8,128]{4,3,2,1,0:T(8,128)(2,1)S(1)}, u32[]{:S(2)}, u32[]{:S(2)}) async-start(f16[4,4,17,8,128]{4,3,2,1,0:T(8,128)(2,1)} %convert_element_type.84), calls=%async_computation.9 | async-start | bytes 1114112 | tf_op jit(solution)/shard_map/all_to_all | solution.py:284
  285.5 4.2 %collective-permute-start.28 = (f32[2]{0:T(128)S(1)}, f32[2]{0:T(128)S(1)}, u32[]{:S(2)}, u32[]{:S(2)}) collective-permute-start(f32[2]{0:T(128)S(1)} %pad_maximum_fusion.4), channel_id=1, source_target_pairs={{0,1},{1,0},{2,3},{3,2},{4,5},{5,4},{6,7},{7,6},{8,9},{9,8},{10,11... | collective-permute-start | bytes 32 | tf_op jit(solution)/shard_map/ppermute | solution.py:295
  285.5 13.2 %all-to-all-start.8 = ((f16[4,4,17,8,128]{4,3,2,1,0:T(8,128)(2,1)}), f16[4,4,17,8,128]{4,3,2,1,0:T(8,128)(2,1)S(1)}, u32[]{:S(2)}, u32[]{:S(2)}) async-start(f16[4,4,17,8,128]{4,3,2,1,0:T(8,128)(2,1)} %convert_element_type.82), calls=%async_computation.8 | async-start | bytes 1114112 | tf_op jit(solution)/shard_map/all_to_all | solution.py:284
  289.8 3.6 %collective-permute-start.29 = (f32[2]{0:T(128)S(1)}, f32[2]{0:T(128)S(1)}, u32[]{:S(2)}, u32[]{:S(2)}) collective-permute-start(f32[2]{0:T(128)S(1)} %fusion.7), channel_id=1, source_target_pairs={{0,2},{1,3},{2,0},{3,1},{4,6},{5,7},{6,4},{7,5},{8,10},{9,11},{10,... | collective-permute-start | bytes 32 | tf_op jit(solution)/shard_map/ppermute | solution.py:295
  311.2 33.1 %all-to-all-start.10 = ((f16[4,33,64,128]{3,2,1,0:T(8,128)(2,1)}), f16[4,33,64,128]{3,2,1,0:T(8,128)(2,1)S(1)}, u32[]{:S(2)}, u32[]{:S(2)}) async-start(f16[4,33,64,128]{3,2,1,0:T(8,128)(2,1)} %convert_element_type.86), calls=%async_computation.10 | async-start | bytes 4325376 | tf_op jit(solution)/shard_map/all_to_all | solution.py:284
  314.8 4.5 %collective-permute-start.30 = (f32[2]{0:T(128)S(1)}, f32[2]{0:T(128)S(1)}, u32[]{:S(2)}, u32[]{:S(2)}) collective-permute-start(f32[2]{0:T(128)S(1)} %fusion.8), channel_id=1, source_target_pairs={{0,4},{1,5},{2,6},{3,7},{4,0},{5,1},{6,2},{7,3},{8,12},{9,13},{10,... | collective-permute-start | bytes 32 | tf_op jit(solution)/shard_map/ppermute | solution.py:295
  319.4 20.9 %collective-permute-start.31 = (f32[2]{0:T(128)S(1)}, f32[2]{0:T(128)S(1)}, u32[]{:S(2)}, u32[]{:S(2)}) collective-permute-start(f32[2]{0:T(128)S(1)} %add.69), channel_id=1, source_target_pairs={{0,8},{1,9},{2,10},{3,11},{4,12},{5,13},{6,14},{7,15},{8,0},{9,1},... | collective-permute-start | bytes 32 | tf_op jit(solution)/shard_map/ppermute | solution.py:295
  340.2 3.6 %collective-permute-start.32 = (f32[2]{0:T(128)S(1)}, f32[2]{0:T(128)S(1)}, u32[]{:S(2)}, u32[]{:S(2)}) collective-permute-start(f32[2]{0:T(128)S(1)} %add.70), channel_id=1, source_target_pairs={{0,16},{1,17},{2,18},{3,19},{4,20},{5,21},{6,22},{7,23},{8,24},{9,... | collective-permute-start | bytes 32 | tf_op jit(solution)/shard_map/ppermute | solution.py:295
  (18 other events, 223.3 us)
